TPU v7x, 32 devices: a whole 2x2x4 slice. The times are simulated.
32 devices in a mesh: gx: 4 (over z), gy: 4 (over y, x), gz: 2 (over core).
Axes of the slice: x: 2, y: 2, z: 4, core: 2. Of those that a mesh axis runs over, the one named last changes fastest.
Arguments:
- right_side: float32 [4, 96, 96, 48], P(None, 'gx', 'gy', 'gz'), may hold values from -6 to 6
- iterate: float32 [4, 96, 96, 48], P(None, 'gx', 'gy', 'gz'), may hold values from -6 to 6
- coefficient: float32 [96, 96, 48], P('gx', 'gy', 'gz'), may hold values from 0.1 to 2
- ordering: int32 [4, 4, 2, 216], P('gx', 'gy', 'gz'), may hold values from 0 to 215, as said below
- leaf_inverse: float32 [4, 4, 2, 125, 125], P('gx', 'gy', 'gz'), may hold values from -2 to 3
- leaf_first: float32 [4, 4, 2, 125, 50], P('gx', 'gy', 'gz'), may hold values from -0.5 to 0.5
- leaf_second: float32 [4, 4, 2, 125, 60], P('gx', 'gy', 'gz'), may hold values from -0.5 to 0.5
- leaf_top: float32 [4, 4, 2, 125, 72], P('gx', 'gy', 'gz'), may hold values from -0.5 to 0.5
- first_inverse: float32 [4, 4, 50, 50], P('gx', 'gy', 'gz'), may hold values from -2 to 3
- first_second: float32 [4, 4, 2, 25, 60], P('gx', 'gy', 'gz'), may hold values from -1.25 to 1.25
- first_top: float32 [4, 4, 2, 25, 72], P('gx', 'gy', 'gz'), may hold values from -1.25 to 1.25
- second_inverse: float32 [4, 240, 240], P('gx', ('gy', 'gz')), may hold values from -2 to 3
- second_top: float32 [4, 4, 2, 30, 72], P('gx', 'gy', 'gz'), may hold values from -1 to 1
- top_inverse: float32 [1152, 1152], P(('gx', 'gy', 'gz')), may hold values from -2 to 3
Outputs:
- correction: float32 [4, 96, 96, 48], P(None, 'gx', 'gy', 'gz')
Inputs may be any that keep to these rules, and one draw needn't show every extreme that they name: `ordering`: each device's row names each of its 216 coarse cells once (cell x 6^2 + y * 6 + z): first the 125 cells with x, y and z all below 5, then the 25 cells with z = 5 and x, y below it, then the 30 cells with y = 5 and x below it, then the 36 cells with x = 5, each group in any order.
All inputs are finite; a program needn't handle non-finite values.
Results may differ from a plain program's by a relative error of at most 0.0003.
Values sent between devices are 32-bit elements; how exact they have to be, the bound alone decides.
A program may use at most 64 MiB of HBM per device.

v0:
```python
import functools

import jax
import jax.numpy as jnp
import numpy as np
from jax import lax
from jax.experimental import pallas as pl
from jax.experimental.pallas import tpu as pltpu
from jax.sharding import PartitionSpec as P

AXES = ("gx", "gy", "gz")
LANES = 128
SIDES = (0, 1, -1)
MESH = pl.DeviceIdType.MESH
f32 = jnp.float32
bf16 = jnp.bfloat16

SHARES = [
    (i, j, k)
    for i in SIDES
    for j in SIDES
    for k in SIDES
    if (i, j, k) != (0, 0, 0) and (i, j, k).count(-1) <= 1
]
RIMS = [(i, j, k) for i in (0, 1) for j in (0, 1) for k in (0, 1) if (i, j, k) != (0, 0, 0)]


def weight(k):
    return max(0, 4 - abs(k)) / 16.0


def weight_beside(k):
    return weight(k - 1) + weight(k + 1)


def single(a, b):
    return jnp.dot(a, b, preferred_element_type=f32)


def single_back(a, b):
    return lax.dot_general(a, b, (((1,), (1,)), ((), ())), preferred_element_type=f32)


def halves(x):
    high = x.astype(bf16)
    return high, (x - high.astype(f32)).astype(bf16)


def stacked(x):
    high = x.astype(bf16).astype(f32)
    return jnp.concatenate([high, x - high], axis=0).astype(bf16)


def dot_exact(a, b, product=single):
    high, low = halves(a)
    return product(high, b) + product(low, b)


def dot(a, b, product=single):
    count = a.shape[0]
    both = product(stacked(a), b[0][...])
    return both[:count] + both[count:] + product(a.astype(bf16), b[1][...])


def dot_back(a, b):
    return dot(a, b, single_back)


def coarse_at(side, row, count):
    if side == 0:
        return row if row < count else None
    if side == 1:
        return count if row == 0 else None
    return -1 if row == count - 1 else None


def restriction(fine, pad, stencil):
    count = fine // 4
    out = np.zeros((3, pad, fine), np.float32)
    for s, side in enumerate(SIDES):
        for row in range(pad):
            at = coarse_at(side, row, count)
            if at is not None:
                for y in range(fine):
                    out[s, row, y] = stencil(y - 4 * at)
    return out


def at_first(table):
    table = table.copy()
    table[0, 0, 0] -= weight(-1)
    return table


def interpolation(fine, pad):
    count = fine // 4
    out = np.zeros((2, fine, pad), np.float32)
    for y in range(fine):
        for at in (y // 4, y // 4 + 1):
            value = 1.0 - abs(y - 4 * at) / 4.0
            if at < count:
                out[0, y, at] = value
            else:
                out[1, y, 0] = value
    return out


def constants(rhs, ny, nz, slabs, pad_y, pad_z, rims):
    plain = restriction(ny, pad_y, weight)
    beside = restriction(ny, pad_y, weight_beside)
    eye = np.eye(slabs, dtype=np.float32)
    rows = np.stack([
        np.concatenate(
            [np.concatenate([np.kron(eye, plain[s]), np.kron(eye, b[s])], 1) for s in range(3)], 0
        )
        for b in (at_first(beside), beside)
    ])

    def over_lanes(table):
        out = np.zeros((3, rhs * nz, LANES), np.float32)
        for s in range(3):
            for r in range(rhs):
                out[s, r * nz:(r + 1) * nz, r * pad_z:(r + 1) * pad_z] = table[s].T
        return np.concatenate(list(out), 1)

    lanes = over_lanes(restriction(nz, pad_z, weight))
    table = restriction(nz, pad_z, weight_beside)
    lanes_beside = np.stack([over_lanes(at_first(table)), over_lanes(table)])
    grow = interpolation(nz, pad_z)
    wide = np.zeros((2, LANES, rhs * nz), np.float32)
    for s in range(2):
        for r in range(rhs):
            wide[s, r * pad_z:(r + 1) * pad_z, r * nz:(r + 1) * nz] = grow[s].T
    eye = np.eye(rims, dtype=np.float32)
    tall_of = interpolation(ny, pad_y)
    tall = np.stack([np.kron(eye, tall_of[s]) for s in range(2)])
    return rows, lanes, lanes_beside, wide, tall


def kernel(
    sizes,
    right_ref, u_ref, coef_ref, order_ref, leaf_raw, leaf_first_raw, leaf_second_raw,
    leaf_top_ref, fs_raw, ft_raw, st_raw, rows_first, rows_second, rows_top,
    mat_rows, mat_lanes, mat_beside, mat_wide, mat_tall,
    out_ref,
    split_leaf, split_links, split_fs, split_ft, split_st, split_rows, left,
    packed, shares, total, share_in, prev, scatter_out, scatter_in, gather_in, whole, pairs,
    picked, ordered, rim, stage,
    share_send, share_recv, prev_send, prev_recv, s_send, s_recv, g_send, g_recv, r_send, r_recv,
):
    rhs, nx, ny, nz = u_ref.shape
    side = nx // 4
    side_y, side_z = ny // 4, nz // 4
    slabs = side + 2
    pad_y, pad_z = sizes["pad_y"], sizes["pad_z"]
    me = {a: lax.axis_index(a) for a in AXES}
    peers = sizes["peers"]
    rows_refs = (rows_first, rows_second, rows_top)
    groups = (("gz",), ("gy", "gz"), AXES)
    shift_axis = ("gz", "gy", "gx")
    counts = [int(np.prod([peers[a] for a in g])) for g in groups]

    def place(group):
        at = 0
        for a in group:
            at = at * peers[a] + me[a]
        return at

    def coords(group, at):
        found = {}
        for a in reversed(group):
            found[a] = at % peers[a]
            at = at // peers[a]
        return {a: found[a] if a in found else me[a] for a in AXES}

    barrier = pltpu.get_barrier_semaphore()
    everyone, myself = counts[2], place(AXES)

    def greet(k, carry):
        pl.semaphore_signal(
            barrier, inc=1, device_id=coords(AXES, (myself + k) % everyone), device_id_type=MESH
        )
        return carry

    lax.fori_loop(1, everyone, greet, 0)

    prev_copies = []
    for level in range(3):
        axis = shift_axis[level]
        target = dict(me)
        target[axis] = (me[axis] + 1) % peers[axis]
        copy = pltpu.make_async_remote_copy(
            src_ref=rows_refs[level], dst_ref=prev[level],
            send_sem=prev_send.at[level], recv_sem=prev_recv.at[level],
            device_id=target, device_id_type=MESH,
        )
        prev_copies.append(copy)

        @pl.when(me[axis] == 0)
        def _():
            prev[level][...] = jnp.zeros(prev[level].shape, f32)

    half = slabs * ny
    for r in range(rhs):
        acc_p = {}
        acc_u = {}

        def add(acc, at, factor, value):
            term = factor * value
            acc[at] = acc[at] + term if at in acc else term

        for x in range(nx):
            u = u_ref[r, x]
            q = right_ref[r, x] - (6.0 + coef_ref[x]) * u
            for at in range(-1, side + 1):
                k = x - 4 * at
                if weight(k):
                    add(acc_p, at, weight(k), q)
                    add(acc_u, at, weight(k), u)
                if at == 0 and x == 0:
                    below = jnp.where(me["gx"] > 0, weight(-1), 0.0)
                    add(acc_p, at, weight(1) + below, u)
                elif weight_beside(k):
                    add(acc_p, at, weight_beside(k), u)
        for at in range(-1, side + 1):
            rows = slice((at + 1) * ny, (at + 2) * ny)
            packed[rows, r * nz:(r + 1) * nz] = acc_p[at]
            rows = slice(half + (at + 1) * ny, half + (at + 2) * ny)
            packed[rows, r * nz:(r + 1) * nz] = acc_u.get(at, jnp.zeros((ny, nz), f32))
    both = packed[...]
    at_y, at_z = jnp.minimum(me["gy"], 1), jnp.minimum(me["gz"], 1)
    high, low = halves(both)
    a = single(mat_rows[at_y], high) + single(mat_rows[at_y], low)
    b = single(mat_rows[1, :, :half], high[half:]) + single(mat_rows[1, :, :half], low[half:])
    c = dot_exact(a, mat_lanes[...]) + dot_exact(b, mat_beside[at_z])
    for s in range(3):
        for t in range(3):
            part = c[s * slabs * pad_y:(s + 1) * slabs * pad_y, t * LANES:(t + 1) * LANES]
            shares[s, t] = part.reshape(slabs, pad_y, LANES)

    def valid(step, sign):
        ok = None
        for a, d in zip(AXES, step):
            if d:
                at = me[a] + sign * d
                this = (at >= 0) & (at < peers[a])
                ok = this if ok is None else ok & this
        return ok

    def toward(step, sign):
        return {a: (me[a] + sign * d + peers[a]) % peers[a] for a, d in zip(AXES, step)}

    pl.semaphore_wait(barrier, everyone - 1)
    for level in range(2):
        @pl.when(me[shift_axis[level]] < peers[shift_axis[level]] - 1)
        def _():
            prev_copies[level].start()

    share_copies = []
    for n, step in enumerate(SHARES):
        dx, dy, dz = step
        cut = {0: pl.ds(1, side), 1: pl.ds(side + 1, 1), -1: pl.ds(0, 1)}[dx]
        copy = pltpu.make_async_remote_copy(
            src_ref=shares.at[SIDES.index(dy), SIDES.index(dz), cut],
            dst_ref=share_in[n],
            send_sem=share_send.at[n], recv_sem=share_recv.at[n],
            device_id=toward(step, 1), device_id_type=MESH,
        )
        share_copies.append(copy)

        @pl.when(valid(step, 1))
        def _():
            copy.start()

    @pl.when(me[shift_axis[2]] < peers[shift_axis[2]] - 1)
    def _():
        prev_copies[2].start()

    total[...] = shares[0, 0, 1:side + 1]

    def keep(where, value):
        where[0][...], where[1][...] = halves(value)

    def rows_of(raw):
        return raw[:, 0, :] if len(raw.shape) == 3 else raw[...]

    spans = [rows.shape[0] for rows in rows_refs]
    seats = [split_rows[level][0].shape[0] // 2 for level in range(3)]

    def keep_rows(level, at, value):
        high, low = halves(value)
        split_rows[level][0][at:at + spans[level], :] = high
        split_rows[level][1][at:at + spans[level], :] = low

    keep(split_leaf, rows_of(leaf_raw))
    for where, raw in zip(split_links, (leaf_first_raw, leaf_second_raw, leaf_top_ref)):
        keep(where, rows_of(raw))
    keep(split_fs, rows_of(fs_raw))
    keep(split_ft, rows_of(ft_raw))
    keep(split_st, rows_of(st_raw))
    for level in range(3):
        for part in split_rows[level]:
            part[...] = jnp.zeros(part.shape, bf16)
        left[level][...] = jnp.zeros(left[level].shape, f32)
        keep_rows(level, 0, rows_of(rows_refs[level]))

    def settle(level):
        axis = shift_axis[level]

        @pl.when(me[axis] > 0)
        def _():
            prev_copies[level].wait_recv()

        keep_rows(level, seats[level], rows_of(prev[level]))

    settle(0)
    settle(1)

    order = order_ref[...].astype(f32)
    first = jnp.floor((order + 0.5) / (side_y * side_z))
    rest = order - first * (side_y * side_z)
    second = jnp.floor((rest + 0.5) / side_z)
    third = rest - second * side_z
    cells = order.shape[1]
    spots = side * pad_y
    row_id = lax.broadcasted_iota(jnp.int32, (spots, cells), 0).astype(f32)
    row_hot = (row_id == first * pad_y + second).astype(f32)
    lane_id = lax.broadcasted_iota(jnp.int32, (LANES, cells), 0).astype(f32)

    def lane_hot(r):
        return (lane_id == third + r * pad_z).astype(f32).astype(bf16)

    for n, step in enumerate(SHARES):
        @pl.when(valid(step, -1))
        def _():
            share_copies[n].wait_recv()
            if step[0] == 0:
                total[...] += share_in[n][...]
            elif step[0] == 1:
                total[0] += share_in[n][0]
            else:
                total[side - 1] += share_in[n][0]

    coarse = total[...].reshape(spots, LANES)
    for r in range(rhs):
        spread = dot_exact(coarse, lane_hot(r))
        picked[r:r + 1, :] = jnp.sum(spread * row_hot, axis=0, keepdims=True)

    leaf = leaf_raw.shape[0]
    starts = [leaf, leaf + spans[0], leaf + spans[0] + spans[1]]
    leaf_solved = dot(picked[:, :leaf], split_leaf)

    def all_slots(buffer, sem, count):
        return pltpu.make_async_copy(
            buffer.at[pl.ds(0, count - 1)], buffer.at[pl.ds(0, count - 1)], sem
        )

    def forward(level, toward_low):
        span, count, group = spans[level], counts[level], groups[level]
        seat = seats[level]
        target = picked[:, starts[level]:starts[level] + span] - toward_low[:, :span]
        left[level][:, :span] = target
        left[level][:, seat:seat + span] = -toward_low[:, span:]
        terms = dot(left[level][...], split_rows[level])
        out, into = scatter_out[level], scatter_in[level]
        for d in range(count):
            out[d, :, :span] = terms[:, d * span:(d + 1) * span]
        mine = place(group)

        def send(k, carry):
            d = (mine + k) % count
            pltpu.make_async_remote_copy(
                src_ref=out.at[d], dst_ref=into.at[mine],
                send_sem=s_send.at[level], recv_sem=s_recv.at[level],
                device_id=coords(group, d), device_id_type=MESH,
            ).start()
            return carry

        lax.fori_loop(1, count, send, 0)
        into[mine] = out[mine]

    def forward_end(level):
        into = scatter_in[level]
        all_slots(into, s_recv.at[level], counts[level]).wait()
        return jnp.sum(into[...], axis=0)[:, :spans[level]]

    def backward(level, gap):
        span, count, group = spans[level], counts[level], groups[level]
        into = gather_in[level]
        own = stage[level]
        mine = place(group)
        own[:, :span] = gap

        def send(k, carry):
            d = (mine + k) % count
            pltpu.make_async_remote_copy(
                src_ref=own, dst_ref=into.at[mine],
                send_sem=g_send.at[level], recv_sem=g_recv.at[level],
                device_id=coords(group, d), device_id_type=MESH,
            ).start()
            return carry

        lax.fori_loop(1, count, send, 0)
        into[mine] = own[...]

    def backward_end(level):
        span, count, seat = spans[level], counts[level], seats[level]
        into = gather_in[level]
        all_slots(into, g_recv.at[level], count).wait()
        full = whole[level]
        for d in range(count):
            full[:, d * span:(d + 1) * span] = into[d, :, :span]
        value = full[...]
        pair = pairs[level]
        solved = dot_back(value, split_rows[level])
        back = solved[:, :span]
        pair[:, :span] = back
        pair[:, span:] = solved[:, seat:seat + span]
        return back, pair[...]

    to_first, to_second, to_top = split_links
    forward(0, dot_back(leaf_solved, to_first))
    second_low = dot_back(leaf_solved, to_second)
    top_low = dot_back(leaf_solved, to_top)
    first_own = forward_end(0)
    forward(1, second_low + dot(first_own, split_fs))
    top_low = top_low + dot(first_own, split_ft)
    settle(2)
    second_own = forward_end(1)
    forward(2, top_low + dot(second_own, split_st))
    top_own = forward_end(2)
    backward(2, top_own)
    top_back, top_pair = backward_end(2)
    backward(1, second_own - dot_back(top_pair, split_st))
    first_gap = first_own - dot_back(top_pair, split_ft)
    leaf_gap = leaf_solved - dot(top_pair, to_top)
    second_back, second_pair = backward_end(1)
    backward(0, first_gap - dot_back(second_pair, split_fs))
    leaf_gap = leaf_gap - dot(second_pair, to_second)
    first_back, first_pair = backward_end(0)
    leaf_back = dot_back(leaf_gap - dot(first_pair, to_first), split_leaf)
    ordered[:, :leaf] = leaf_back
    ordered[:, starts[0]:starts[1]] = first_back
    ordered[:, starts[1]:starts[2]] = second_back
    ordered[:, starts[2]:] = top_back

    cells_back = None
    for r in range(rhs):
        term = dot_exact(row_hot * ordered[r:r + 1, :], lane_hot(r), single_back)
        cells_back = term if cells_back is None else cells_back + term
    rim[0, 0, 0:side] = cells_back.reshape(side, pad_y, LANES)

    rim_copies = []
    for n, step in enumerate(RIMS):
        dx, dy, dz = step
        source = rim.at[0, 0, pl.ds(0, 1 if dx else side)]
        landing = rim.at[dy, dz, pl.ds(side, 1) if dx else pl.ds(0, side)]
        copy = pltpu.make_async_remote_copy(
            src_ref=source, dst_ref=landing,
            send_sem=r_send.at[n], recv_sem=r_recv.at[n],
            device_id=toward(step, -1), device_id_type=MESH,
        )
        rim_copies.append(copy)

        @pl.when(valid(step, -1))
        def _():
            copy.start()

    for n, step in enumerate(RIMS):
        dx, dy, dz = step
        here = valid(step, 1)

        @pl.when(here)
        def _():
            rim_copies[n].wait_recv()

        @pl.when(jnp.logical_not(here))
        def _():
            if dx:
                rim[dy, dz, side] = jnp.zeros((pad_y, LANES), f32)
            else:
                rim[dy, dz, 0:side] = jnp.zeros((side, pad_y, LANES), f32)

    tall_rows = (side + 1) * pad_y
    grown = None
    for s in range(2):
        wide = dot_exact(rim[s, 0].reshape(tall_rows, LANES), mat_wide[0])
        wide = wide + dot_exact(rim[s, 1].reshape(tall_rows, LANES), mat_wide[1])
        high, low = halves(wide)
        term = single(mat_tall[s], high) + single(mat_tall[s], low)
        grown = term if grown is None else grown + term
    out_ref[...] = grown

    for level in range(3):
        axis = shift_axis[level]

        @pl.when(me[axis] < peers[axis] - 1)
        def _():
            prev_copies[level].wait_send()

        all_slots(scatter_out[level], s_send.at[level], counts[level]).wait()
        all_slots(gather_in[level], g_send.at[level], counts[level]).wait()
    for n, step in enumerate(SHARES):
        @pl.when(valid(step, 1))
        def _():
            share_copies[n].wait_send()
    for n, step in enumerate(RIMS):
        @pl.when(valid(step, -1))
        def _():
            rim_copies[n].wait_send()


def spread_kernel(grown_ref, out_ref):
    rhs, nx, ny, nz = out_ref.shape
    side = nx // 4
    for r in range(rhs):
        slices = [
            grown_ref[at * ny:(at + 1) * ny, r * nz:(r + 1) * nz] for at in range(side + 1)
        ]
        for x in range(nx):
            at, k = x // 4, x % 4
            if k == 0:
                out_ref[r, x] = slices[at]
            else:
                out_ref[r, x] = (1 - k / 4) * slices[at] + (k / 4) * slices[at + 1]


def per_device(peers, right_side, iterate, coefficient, ordering, leaf_inverse, leaf_first,
               leaf_second, leaf_top, first_inverse, first_second, first_top, second_inverse,
               second_top, top_inverse):
    rhs, nx, ny, nz = iterate.shape
    side = nx // 4
    slabs = side + 2
    pad_y = -(-(ny // 4) // 8) * 8
    pad_z = LANES // rhs // 4 if nz // 4 <= LANES // rhs // 4 else LANES // rhs
    mats = constants(rhs, ny, nz, slabs, pad_y, pad_z, side + 1)
    flip = lambda m: jnp.swapaxes(m, -1, -2)
    flat = lambda m: m.reshape(m.shape[-2:])
    single_rows = lambda m: m.reshape(m.shape[-2], 1, m.shape[-1])
    rows = [single_rows(first_inverse), single_rows(second_inverse), top_inverse]
    spans = [m.shape[0] for m in rows]
    widths = [m.shape[-1] for m in rows]
    counts = [w // s for w, s in zip(widths, spans)]
    seats = [-(-s // 16) * 16 for s in spans]
    leaf = leaf_inverse.shape[-1]
    cells = ordering.shape[-1]
    vmem = lambda *shape: pltpu.VMEM(shape, f32)
    split = lambda *shape: [pltpu.VMEM(shape, bf16)] * 2
    dma = lambda n: pltpu.SemaphoreType.DMA((n,))
    tile = (pad_y, LANES)
    sizes = {"peers": peers, "pad_y": pad_y, "pad_z": pad_z}
    operands = (
        right_side, iterate, coefficient, ordering.reshape(1, cells), single_rows(leaf_inverse),
        single_rows(flip(leaf_first)), single_rows(flip(leaf_second)), flat(flip(leaf_top)),
        single_rows(first_second), single_rows(first_top), single_rows(second_top), *rows,
        *[jnp.asarray(m, bf16) for m in mats],
    )
    in_vmem = pl.BlockSpec(memory_space=pltpu.VMEM)
    grown = pl.pallas_call(
        functools.partial(kernel, sizes),
        out_shape=jax.ShapeDtypeStruct(((side + 1) * ny, rhs * nz), f32),
        in_specs=jax.tree.map(lambda _: in_vmem, operands),
        out_specs=in_vmem,
        scratch_shapes=[
            split(leaf, leaf),
            [split(2 * s, leaf) for s in spans],
            split(spans[0], 2 * spans[1]),
            split(spans[0], 2 * spans[2]),
            split(spans[1], 2 * spans[2]),
            [split(2 * seat, w) for seat, w in zip(seats, widths)],
            [vmem(rhs, 2 * seat) for seat in seats],
            vmem(2 * slabs * ny, rhs * nz),
            vmem(3, 3, slabs, *tile),
            vmem(side, *tile),
            [vmem(side if step[0] == 0 else 1, *tile) for step in SHARES],
            [vmem(*m.shape) for m in rows],
            [vmem(n, rhs, LANES) for n in counts],
            [vmem(n, rhs, LANES) for n in counts],
            [vmem(n, rhs, LANES) for n in counts],
            [vmem(rhs, w) for w in widths],
            [vmem(rhs, 2 * s) for s in spans],
            vmem(rhs, cells),
            vmem(rhs, cells),
            vmem(2, 2, side + 1, *tile),
            [vmem(rhs, LANES) for _ in rows],
            dma(len(SHARES)), dma(len(SHARES)), dma(3), dma(3), dma(3), dma(3), dma(3), dma(3),
            dma(len(RIMS)), dma(len(RIMS)),
        ],
        compiler_params=pltpu.CompilerParams(has_side_effects=True, collective_id=0),
    )(*operands)
    return pl.pallas_call(
        spread_kernel,
        out_shape=jax.ShapeDtypeStruct(iterate.shape, f32),
        in_specs=[in_vmem],
        out_specs=in_vmem,
    )(grown)


def solution(mesh):
    peers = dict(mesh.shape)
    return jax.shard_map(
        functools.partial(per_device, peers),
        mesh=mesh,
        in_specs=(
            P(None, "gx", "gy", "gz"),
            P(None, "gx", "gy", "gz"),
            P("gx", "gy", "gz"),
            P("gx", "gy", "gz", None),
            P("gx", "gy", "gz", None, None),
            P("gx", "gy", "gz", None, None),
            P("gx", "gy", "gz", None, None),
            P("gx", "gy", "gz", None, None),
            P("gx", "gy", "gz", None),
            P("gx", "gy", "gz", None, None),
            P("gx", "gy", "gz", None, None),
            P("gx", ("gy", "gz"), None),
            P("gx", "gy", "gz", None, None),
            P(("gx", "gy", "gz"), None),
        ),
        out_specs=P(None, "gx", "gy", "gz"),
        check_vma=False,
    )
```

profile of v0, /device:TPU:0, one launch (start us, length us, event | category | flops | bytes accessed | tf_op | source)
XLA Modules:
  0.0 42.0 jit_solution(10307044753061611000)
XLA Ops:
  0.0 39.8 %shard_map.181.grown_ref = f32[168,96]{1,0:T(8,128)} custom-call(f32[4,24,24,24]{3,2,1,0:T(8,128)} %right_ref.1, f32[4,24,24,24]{3,2,1,0:T(8,128)} %u_ref.1, f32[24,24,24]{2,1,0:T(8,128)} %coef_ref.1, s32[1,216]{1,0:T(1,128)} %bitcast.29, f32[125,1,125]{2,1,0:T(1,128)} %bitcast.20, f32[50,1,125]{2,1,0:T(1,128)} %bitcast.24, f32[60,1,125]{2,1,0:T(1,128)} %bitcast.22, ...), custom_call_target="tpu_custom_call" | custom-call | tf_op jit(solution)/shard_map/pallas_call | solution.py:559
  39.8 2.2 %shard_map.182 = f32[4,24,24,24]{3,2,1,0:T(8,128)} custom-call(f32[168,96]{1,0:T(8,128)} %shard_map.181.grown_ref), custom_call_target="tpu_custom_call" | custom-call | tf_op jit(solution)/shard_map/pallas_call | solution.py:591
where the time goes:
time: 42.2 us; the launch traced here: 42 us
  Pallas kernels  42 us (100%)
    pallas_call x1, Pallas kernels, per_device(): pl.pallas_call(functools.partial(kernel, sizes), out_shape=jax.ShapeDtype...  39.8 us
    pallas_call x1, Pallas kernels, per_device(): pl.pallas_call(spread_kernel, out_shape=jax.ShapeDtypeStruct(iterate.shap...  2.2 us

commit v1 on v0

v1 whole, which is shorter than its diff:
```python
import functools
import itertools

import jax
import jax.numpy as jnp
import numpy as np
from jax import lax
from jax.experimental import pallas as pl
from jax.experimental.pallas import tpu as pltpu
from jax.sharding import PartitionSpec as P

AXES = ("gx", "gy", "gz")
LANES = 128
TILE = 8
PITCH = 32
UNROLL = 64
SIDES = (0, 1, -1)
MESH = pl.DeviceIdType.MESH
f32 = jnp.float32
bf16 = jnp.bfloat16

SHARES = [
    (i, j, k)
    for i in SIDES
    for j in SIDES
    for k in SIDES
    if (i, j, k) != (0, 0, 0) and (i, j, k).count(-1) <= 1
]
RIMS = [(i, j, k) for i in (0, 1) for j in (0, 1) for k in (0, 1) if (i, j, k) != (0, 0, 0)]


def up_to(n, unit):
    return -(-n // unit) * unit


def weight(k):
    return max(0, 4 - abs(k)) / 16.0


def weight_beside(k):
    return weight(k - 1) + weight(k + 1)


def single(a, b):
    return jnp.dot(a, b, preferred_element_type=f32)


def single_back(a, b):
    return lax.dot_general(a, b, (((1,), (1,)), ((), ())), preferred_element_type=f32)


def halves(x):
    high = x.astype(bf16)
    return high, (x - high.astype(f32)).astype(bf16)


def stacked(x):
    high = x.astype(bf16).astype(f32)
    return jnp.concatenate([high, x - high], axis=0).astype(bf16)


def dot_exact(a, b, product=single):
    count = a.shape[0]
    both = product(stacked(a), b)
    return both[:count] + both[count:]


def dot(a, b, product=single):
    count = a.shape[0]
    both = product(stacked(a), b[0][...])
    return both[:count] + both[count:] + product(a.astype(bf16), b[1][...])


def dot_back(a, b):
    return dot(a, b, single_back)


def coarse_at(side, row, count):
    if side == 0:
        return row if row < count else None
    if side == 1:
        return count if row == 0 else None
    return -1 if row == count - 1 else None


def restriction(fine, pad, stencil):
    count = fine // 4
    out = np.zeros((3, pad, fine), np.float32)
    for s, side in enumerate(SIDES):
        for row in range(pad):
            at = coarse_at(side, row, count)
            if at is not None:
                for y in range(fine):
                    out[s, row, y] = stencil(y - 4 * at)
    return out


def at_first(table):
    table = table.copy()
    table[0, 0, 0] -= weight(-1)
    return table


def interpolation(fine, pad):
    count = fine // 4
    out = np.zeros((2, fine, pad), np.float32)
    for y in range(fine):
        for at in (y // 4, y // 4 + 1):
            value = 1.0 - abs(y - 4 * at) / 4.0
            if at < count:
                out[0, y, at] = value
            else:
                out[1, y, 0] = value
    return out


def constants(rhs, ny, nz, side, pad_y, pad_z):
    slabs = side + 2
    edge_rows = up_to(slabs, TILE)
    last = ny // 4 - 1
    eye = np.eye(slabs, dtype=np.float32)
    eye_edge = np.eye(edge_rows, slabs, dtype=np.float32)

    def over_rows(table):
        return np.concatenate([
            np.kron(eye, table[0]),
            np.kron(eye_edge, table[1][0:1]),
            np.kron(eye_edge, table[2][last:last + 1]),
        ], 0)

    plain = over_rows(restriction(ny, pad_y, weight))
    beside = restriction(ny, pad_y, weight_beside)
    rows = np.stack([
        np.concatenate([plain, over_rows(b)], 1) for b in (at_first(beside), beside)
    ])

    def over_lanes(table):
        out = np.zeros((3, rhs * nz, LANES), np.float32)
        for s in range(3):
            for r in range(rhs):
                out[s, r * nz:(r + 1) * nz, r * pad_z:(r + 1) * pad_z] = table[s].T
        return np.concatenate(list(out), 1)

    lanes = over_lanes(restriction(nz, pad_z, weight))
    table = restriction(nz, pad_z, weight_beside)
    lanes_beside = np.stack([over_lanes(at_first(table)), over_lanes(table)])
    grow = interpolation(nz, pad_z)
    wide = np.zeros((2, LANES, rhs * nz), np.float32)
    for s in range(2):
        for r in range(rhs):
            wide[s, r * pad_z:(r + 1) * pad_z, r * nz:(r + 1) * nz] = grow[s].T
    wide = wide.reshape(2 * LANES, rhs * nz)
    tall_of = interpolation(ny, pad_y)
    slab_rows = side * pad_y
    face_rows = up_to(side, TILE)
    tall = np.zeros(((side + 1) * ny, slab_rows + pad_y + 2 * face_rows), np.float32)
    for at in range(side + 1):
        here = slice(at * ny, (at + 1) * ny)
        tall[here, at * pad_y:(at + 1) * pad_y] = tall_of[0]
        beyond = slab_rows + pad_y + (at if at < side else face_rows)
        tall[here, beyond] = tall_of[1][:, 0]
    return rows, lanes, lanes_beside, wide, tall


def kernel(
    sizes,
    right_ref, u_ref, coef_ref, order_ref, leaf_ref, first_ref, second_ref, top_ref,
    fs_ref, ft_ref, st_ref, rows_first, rows_second, rows_top,
    mat_rows, mat_lanes, mat_beside, mat_wide, mat_tall,
    out_ref,
    right_in, u_in, coef_in, order_in, leaf_in, first_in, second_in, top_in,
    fs_in, ft_in, st_in, rows_in, m_rows, m_lanes, m_beside, m_wide, m_tall,
    leaf_split, link_split, fs_seat, ftst_seat, row_seat, rows0, rows1, big, w0, zed, kay,
    packed, shares, share_in, prev, scatter_out, scatter_in, gather_in, top_all, val,
    picked, slots, order_seat, ordered, rim, face, stage, k_own, k_all,
    in_sem, share_send, share_recv, prev_send, prev_recv, k_sem, s_send, s_recv, g_send, g_recv,
    r_send, r_recv,
):
    rhs, nx, ny, nz = u_in.shape
    side = nx // 4
    side_y, side_z = ny // 4, nz // 4
    slabs = side + 2
    pad_y, pad_z = sizes["pad_y"], sizes["pad_z"]
    spans, seats, widths = sizes["spans"], sizes["seats"], sizes["widths"]
    leaf = leaf_in.shape[0]
    at_first_level, at_second, at_top = sizes["starts"]
    peers = sizes["peers"]
    me = {a: lax.axis_index(a) for a in AXES}
    groups = (("gz",), ("gy", "gz"), AXES)
    shift_axis = ("gz", "gy", "gx")
    counts = [int(np.prod([peers[a] for a in g])) for g in groups]
    n_gz = peers["gz"]

    def place(group):
        at = 0
        for a in group:
            at = at * peers[a] + me[a]
        return at

    def coords(group, at):
        found = {}
        for a in reversed(group):
            found[a] = at % peers[a]
            at = at // peers[a]
        return {a: found[a] if a in found else me[a] for a in AXES}

    turned = {a: [me[a]] for a in AXES}
    for a in AXES:
        for k in range(1, peers[a]):
            at = me[a] + k
            turned[a].append(jnp.where(at >= peers[a], at - peers[a], at))

    def for_others(group, send):
        count = int(np.prod([peers[a] for a in group]))
        if count <= UNROLL:
            for steps in itertools.product(*[range(peers[a]) for a in group]):
                if any(steps):
                    target = dict(me)
                    at = 0
                    for a, k in zip(group, steps):
                        target[a] = turned[a][k]
                        at = at * peers[a] + turned[a][k]
                    send(target, at)
        else:
            mine = place(group)

            def step(k, carry):
                at = (mine + k) % count
                send(coords(group, at), at)
                return carry

            lax.fori_loop(1, count, step, 0)

    barrier = pltpu.get_barrier_semaphore()
    everyone = counts[2]

    def greet(target, at):
        pl.semaphore_signal(barrier, inc=1, device_id=target, device_id_type=MESH)

    at_y, at_z = jnp.minimum(me["gy"], 1), jnp.minimum(me["gz"], 1)
    loads = {}

    def load(name, source, into):
        loads[name] = pltpu.make_async_copy(source, into, in_sem.at[len(loads)])
        loads[name].start()

    load("coef", coef_ref, coef_in)
    for r in range(rhs):
        load(("u", r), u_ref.at[r], u_in.at[r])
        load(("right", r), right_ref.at[r], right_in.at[r])
    load("m_rows", mat_rows.at[at_y], m_rows)
    load("m_lanes", mat_lanes, m_lanes)
    load("m_beside", mat_beside.at[at_z], m_beside)
    row_sources = (rows_first, rows_second, rows_top)
    for level in range(3):
        load(("rows", level), row_sources[level], rows_in[level])
    load("leaf", leaf_ref, leaf_in)
    load("first", first_ref, first_in)
    load("second", second_ref, second_in)
    load("top", top_ref, top_in)
    load("order", order_ref, order_in)
    load("fs", fs_ref, fs_in)
    load("ft", ft_ref, ft_in)
    load("st", st_ref, st_in)
    load("m_wide", mat_wide, m_wide)
    load("m_tall", mat_tall, m_tall)

    def clear(ref):
        ref[...] = jnp.zeros(ref.shape, ref.dtype)

    for buffer in share_in:
        clear(buffer)
    clear(rim)
    for_others(AXES, greet)

    for level in range(3):
        @pl.when(me[shift_axis[level]] == 0)
        def _():
            clear(prev[level])
    clear(k_own)
    for level in range(2):
        clear(scatter_out[level])

    half = slabs * ny
    loads["coef"].wait()
    for r in range(rhs):
        loads["u", r].wait()
        loads["right", r].wait()
        acc_p = {}
        acc_u = {}

        def add(acc, at, factor, value):
            term = factor * value
            acc[at] = acc[at] + term if at in acc else term

        for x in range(nx):
            u = u_in[r, x]
            q = right_in[r, x] - (6.0 + coef_in[x]) * u
            for at in range(-1, side + 1):
                k = x - 4 * at
                if weight(k):
                    add(acc_p, at, weight(k), q)
                    add(acc_u, at, weight(k), u)
                if at == 0 and x == 0:
                    below = jnp.where(me["gx"] > 0, weight(-1), 0.0)
                    add(acc_p, at, weight(1) + below, u)
                elif weight_beside(k):
                    add(acc_p, at, weight_beside(k), u)
        for at in range(-1, side + 1):
            rows = slice((at + 1) * ny, (at + 2) * ny)
            packed[rows, r * nz:(r + 1) * nz] = acc_p[at]
            rows = slice(half + (at + 1) * ny, half + (at + 2) * ny)
            packed[rows, r * nz:(r + 1) * nz] = acc_u.get(at, jnp.zeros((ny, nz), f32))
    loads["m_rows"].wait()
    loads["m_lanes"].wait()
    loads["m_beside"].wait()
    high, low = halves(packed[...])
    a = single(m_rows[...], high) + single(m_rows[...], low)
    b = single(m_rows[:, :half], high[half:]) + single(m_rows[:, :half], low[half:])
    c = dot_exact(a, m_lanes[...]) + dot_exact(b, m_beside[...])
    for t in range(3):
        shares[t] = c[:, t * LANES:(t + 1) * LANES]

    def valid(step, sign):
        ok = None
        for a, d in zip(AXES, step):
            if d:
                at = me[a] + sign * d
                this = (at >= 0) & (at < peers[a])
                ok = this if ok is None else ok & this
        return ok

    def toward(step, sign):
        return {a: (me[a] + sign * d + peers[a]) % peers[a] for a, d in zip(AXES, step)}

    for level in range(3):
        loads["rows", level].wait()
    pl.semaphore_wait(barrier, everyone - 1)

    edge_rows = up_to(slabs, TILE)
    main = side * pad_y
    share_copies = []
    for n, step in enumerate(SHARES):
        dx, dy, dz = step
        if dy == 0:
            cut = {0: pl.ds(pad_y, main), 1: pl.ds((side + 1) * pad_y, pad_y), -1: pl.ds(0, pad_y)}[dx]
        else:
            cut = pl.ds(slabs * pad_y + (edge_rows if dy < 0 else 0), edge_rows)
        copy = pltpu.make_async_remote_copy(
            src_ref=shares.at[SIDES.index(dz), cut], dst_ref=share_in[n],
            send_sem=share_send.at[n], recv_sem=share_recv.at[n],
            device_id=toward(step, 1), device_id_type=MESH,
        )
        share_copies.append(copy)

        @pl.when(valid(step, 1))
        def _():
            copy.start()

    prev_copies = []
    for level in range(3):
        axis = shift_axis[level]
        target = dict(me)
        target[axis] = (me[axis] + 1) % peers[axis]
        copy = pltpu.make_async_remote_copy(
            src_ref=rows_in[level], dst_ref=prev[level],
            send_sem=prev_send.at[level], recv_sem=prev_recv.at[level],
            device_id=target, device_id_type=MESH,
        )
        prev_copies.append(copy)

        @pl.when(me[axis] < peers[axis] - 1)
        def _():
            copy.start()

    def keep(where, value, rows=None):
        high, low = halves(value)
        if rows is None:
            where[0][...], where[1][...] = high, low
        else:
            where[0][rows, :] = high
            where[1][rows, :] = low

    def rows_of(raw):
        return raw[:, 0, :] if len(raw.shape) == 3 else raw[...]

    for name in ("leaf", "first", "second", "top", "fs", "ft", "st", "order"):
        loads[name].wait()
    keep(leaf_split, rows_of(leaf_in))
    link_at = [0, 2 * seats[0], 2 * (seats[0] + seats[1])]
    for pair in (link_split, rows0, rows1, big, w0):
        for part in pair:
            clear(part)
    for level, raw in enumerate((first_in, second_in, top_in)):
        value = rows_of(raw)
        span = spans[level]
        for s in range(2):
            at = link_at[level] + s * seats[level]
            keep(link_split, value[s * span:(s + 1) * span], slice(at, at + span))

    clear(fs_seat)
    clear(ftst_seat)
    for s in range(2):
        span, seat = spans[1], seats[1]
        fs_seat[:spans[0], s * seat:s * seat + span] = rows_of(fs_in)[:, s * span:(s + 1) * span]
        span, seat = spans[2], seats[2]
        ftst_seat[:spans[1], s * seat:s * seat + span] = rows_of(st_in)[:, s * span:(s + 1) * span]
        ftst_seat[PITCH:PITCH + spans[0], s * seat:s * seat + span] = (
            rows_of(ft_in)[:, s * span:(s + 1) * span]
        )

    clear(order_seat)
    starts = (0, leaf, leaf + spans[0], leaf + spans[0] + spans[1], order_in.shape[1])
    seated = (0, at_first_level, at_second, at_top)
    order_seat[...] = jnp.full(order_seat.shape, -1e6, f32)
    for begin, end, at in zip(starts, starts[1:], seated):
        order_seat[:, at:at + end - begin] = order_in[:, begin:end].astype(f32)
    order = order_seat[...]
    first = jnp.floor((order + 0.5) / (side_y * side_z))
    rest = order - first * (side_y * side_z)
    second = jnp.floor((rest + 0.5) / side_z)
    third = rest - second * side_z
    cells = order.shape[1]

    def row_iota(count):
        return lax.broadcasted_iota(jnp.int32, (count, cells), 0).astype(f32)

    main_hot = (row_iota(main) == first * pad_y + second).astype(f32)
    edge_id = row_iota(edge_rows)
    near = (edge_id == first + 1) | ((edge_id == slabs - 1) & (first == 0)) | (
        (edge_id == 0) & (first == side - 1)
    )
    pick_hot = jnp.concatenate([
        main_hot,
        (near & (second == 0)).astype(f32),
        (near & (second == side_y - 1)).astype(f32),
    ], 0)
    face_rows = face.shape[0]
    face_hot = ((row_iota(face_rows) == first) & (second == 0)).astype(f32)
    back_hot = jnp.concatenate([main_hot, face_hot], 0)
    lane_id = lax.broadcasted_iota(jnp.int32, (LANES, cells), 0).astype(f32)

    def lane_hot(r):
        return (lane_id == third + r * pad_z).astype(f32).astype(bf16)

    def wait_prev(level):
        @pl.when(me[shift_axis[level]] > 0)
        def _():
            prev_copies[level].wait_recv()

    def seat_lanes(value, level):
        span = spans[level]
        row_seat[level][...] = jnp.zeros(row_seat[level].shape, f32)
        for d in range(counts[level]):
            row_seat[level][:, d * PITCH:d * PITCH + span] = value[:, d * span:(d + 1) * span]
        return row_seat[level][...]

    links = dot_back(rows_of(leaf_in), link_split)
    wait_prev(0)
    own0 = seat_lanes(rows_of(rows_in[0]), 0)
    keep(rows0, own0, slice(0, spans[0]))
    keep(w0, own0, slice(at_first_level, at_first_level + spans[0]))
    keep(rows0, seat_lanes(rows_of(prev[0]), 0), slice(seats[0], seats[0] + spans[0]))
    e0 = dot(links[:, :2 * seats[0]], rows0)
    keep(w0, -e0, slice(0, leaf))
    wait_prev(1)
    own1 = seat_lanes(rows_of(rows_in[1]), 1)
    keep(rows1, own1, slice(0, spans[1]))
    keep(rows1, seat_lanes(rows_of(prev[1]), 1), slice(seats[1], seats[1] + spans[1]))
    k_own[...] = dot(fs_seat[...], rows1)
    mine0 = place(groups[0])

    def send_k(target, at):
        pltpu.make_async_remote_copy(
            src_ref=k_own, dst_ref=k_all.at[mine0],
            send_sem=k_sem.at[0], recv_sem=k_sem.at[1],
            device_id=target, device_id_type=MESH,
        ).start()

    for_others(groups[0], send_k)
    k_all[mine0] = k_own[...]

    def all_slots(buffer, sem, count):
        return pltpu.make_async_copy(
            buffer.at[pl.ds(0, count - 1)], buffer.at[pl.ds(0, count - 1)], sem
        )

    e1 = dot(links[:, 2 * seats[0]:2 * (seats[0] + seats[1])], rows1)
    w1_value = jnp.concatenate([
        -e1, jnp.zeros((at_second - leaf, e1.shape[1]), f32), own1,
        jnp.zeros((at_top - at_second - spans[1], e1.shape[1]), f32),
    ], 0)
    all_slots(k_all, k_sem.at[1], n_gz).wait()
    keep(kay, k_all[...].reshape(n_gz * PITCH, k_own.shape[1]))
    w0_value = w0[0][...].astype(f32) + w0[1][...].astype(f32)
    gap_width = widths[1]
    zed_value = w1_value - dot(w0_value, kay)
    high, low = halves(zed_value)
    zed[0][:, :gap_width], zed[1][:, :gap_width] = high, low
    zed[0][:, gap_width:], zed[1][:, gap_width:] = w0[0][...], w0[1][...]

    received = {}
    for n, step in enumerate(SHARES):
        @pl.when(valid(step, -1))
        def _():
            share_copies[n].wait_recv()
    for n, step in enumerate(SHARES):
        dx, dy, dz = step
        received[dx, dy] = received[dx, dy] + share_in[n][...] if (dx, dy) in received else share_in[n][...]

    total = shares[0, pad_y:pad_y + main] + received[0, 0]
    pieces = [total[:pad_y] + received[1, 0], total[pad_y:main - pad_y], total[main - pad_y:] + received[-1, 0]]
    edge_lane = lax.broadcasted_iota(jnp.int32, (edge_rows, LANES), 0)
    inside = (edge_lane >= 1) & (edge_lane <= side)
    for dy in (1, -1):
        tile = jnp.where(inside, received[0, dy], 0.0)
        tile = tile + jnp.where(edge_lane == slabs - 1, received[1, dy], 0.0)
        if (-1, dy) in received:
            tile = tile + jnp.where(edge_lane == 0, received[-1, dy], 0.0)
        pieces.append(tile)
    coarse = jnp.concatenate(pieces, 0)
    for r in range(rhs):
        spread = dot_exact(coarse, lane_hot(r))
        picked[r:r + 1, :] = jnp.sum(spread * pick_hot, axis=0, keepdims=True)

    def scatter(level, terms, pitch, lane):
        span, group = spans[level], groups[level]
        out, into = scatter_out[level], scatter_in[level]
        for d in range(counts[level]):
            out[d, :, lane:lane + span] = terms[:, d * pitch:d * pitch + span]
        mine = place(group)

        def send(target, d):
            pltpu.make_async_remote_copy(
                src_ref=out.at[d], dst_ref=into.at[mine],
                send_sem=s_send.at[level], recv_sem=s_recv.at[level],
                device_id=target, device_id_type=MESH,
            ).start()

        for_others(group, send)
        into[mine] = out[mine]

    def scatter_end(level):
        into = scatter_in[level]
        all_slots(into, s_recv.at[level], counts[level]).wait()
        return jnp.sum(into[...], axis=0)

    def gather(level, value):
        group = groups[level]
        into, own = gather_in[level], stage[level]
        mine = place(group)
        own[...] = value

        def send(target, d):
            pltpu.make_async_remote_copy(
                src_ref=own, dst_ref=into.at[mine],
                send_sem=g_send.at[level], recv_sem=g_recv.at[level],
                device_id=target, device_id_type=MESH,
            ).start()

        for_others(group, send)
        into[mine] = own[...]

    def gather_end(level):
        into = gather_in[level]
        all_slots(into, g_recv.at[level], counts[level]).wait()
        return into

    below_top = picked[:, :at_top]
    scatter(1, dot(below_top, (zed[0][:, :gap_width], zed[1][:, :gap_width])), PITCH, 0)
    scatter(0, dot(below_top, w0), PITCH, PITCH)

    wait_prev(2)
    keep(big, rows_of(rows_in[2]), slice(0, spans[2]))
    keep(big, rows_of(prev[2]), slice(seats[2], seats[2] + spans[2]))
    pair2 = 2 * seats[2]
    rows2 = (big[0].at[pl.ds(0, pair2)], big[1].at[pl.ds(0, pair2)])
    queue = slice(LANES, LANES + 2 * PITCH)
    keep(big, dot(ftst_seat[...], rows2), queue)
    leaf_rhs = picked[:, :leaf]
    tops = dot(leaf_rhs, halves(links[:, 2 * (seats[0] + seats[1]):]))
    slots[...] = -tops
    slots[:, :spans[2]] = picked[:, at_top:at_top + spans[2]] - tops[:, :spans[2]]
    base2 = dot(slots[...], rows2)
    first_own = scatter_end(0)
    queue_rows = (big[0].at[queue], big[1].at[queue])
    base2 = base2 - dot(first_own[:, :2 * PITCH], queue_rows)
    leaf_solved = dot(leaf_rhs, leaf_split)
    second_own = scatter_end(1)
    scatter(2, base2 - dot(second_own[:, :2 * PITCH], queue_rows), spans[2], 0)
    both_own = (first_own + second_own)[:, :2 * PITCH]
    top_own = scatter_end(2)
    gather(2, top_own)
    into = gather_end(2)
    for d in range(counts[2]):
        top_all[:, d * spans[2]:(d + 1) * spans[2]] = into[d, :, :spans[2]]
    solved = dot_back(top_all[...], big)
    gather(1, jnp.concatenate([
        both_own - solved[:, LANES:LANES + 2 * PITCH], jnp.zeros((rhs, LANES - 2 * PITCH), f32)
    ], 1))
    top_link = (link_split[0].at[pl.ds(link_at[2], pair2)], link_split[1].at[pl.ds(link_at[2], pair2)])
    base = dot_back(leaf_solved - dot(solved[:, :pair2], top_link), leaf_split)

    for level in range(3):
        @pl.when(me[shift_axis[level]] < peers[shift_axis[level]] - 1)
        def _():
            prev_copies[level].wait_send()

        all_slots(scatter_out[level], s_send.at[level], counts[level]).wait()
    all_slots(k_all, k_sem.at[0], n_gz).wait()
    all_slots(gather_in[2], g_send.at[2], counts[2]).wait()
    for n, step in enumerate(SHARES):
        @pl.when(valid(step, 1))
        def _():
            share_copies[n].wait_send()

    into = gather_end(1)
    clear(val)
    for d in range(counts[1]):
        val[:, d * PITCH:d * PITCH + spans[1]] = into[d, :, :spans[1]]
    for d in range(n_gz):
        at = gap_width + d * PITCH
        val[:, at:at + spans[0]] = into[me["gy"] * n_gz + d, :, PITCH:PITCH + spans[0]]
    back = dot_back(val[...], zed)
    clear(ordered)
    ordered[:, :at_top] = back
    ordered[:, :leaf] = back[:, :leaf] + base
    ordered[:, at_top:at_top + spans[2]] = solved[:, :spans[2]]

    cells_back = None
    for r in range(rhs):
        term = dot_exact(back_hot * ordered[r:r + 1, :], lane_hot(r), single_back)
        cells_back = term if cells_back is None else cells_back + term
    rim[0, 0:main] = cells_back[:main]
    face[...] = cells_back[main:]

    rim_copies = []
    for n, step in enumerate(RIMS):
        dx, dy, dz = step
        if dy:
            source, at = face, main + pad_y + (face_rows if dx else 0)
        elif dx:
            source, at = rim.at[0, pl.ds(0, pad_y)], main
        else:
            source, at = rim.at[0, pl.ds(0, main)], 0
        rows = face_rows if dy else (pad_y if dx else main)
        copy = pltpu.make_async_remote_copy(
            src_ref=source, dst_ref=rim.at[dz, pl.ds(at, rows)],
            send_sem=r_send.at[n], recv_sem=r_recv.at[n],
            device_id=toward(step, -1), device_id_type=MESH,
        )
        rim_copies.append(copy)

        @pl.when(valid(step, -1))
        def _():
            copy.start()

    loads["m_wide"].wait()
    loads["m_tall"].wait()
    all_slots(gather_in[1], g_send.at[1], counts[1]).wait()
    for n, step in enumerate(RIMS):
        @pl.when(valid(step, 1))
        def _():
            rim_copies[n].wait_recv()

    wide = dot_exact(jnp.concatenate([rim[0], rim[1]], 1), m_wide[...])
    high, low = halves(wide)
    out_ref[...] = single(m_tall[...], high) + single(m_tall[...], low)

    for n, step in enumerate(RIMS):
        @pl.when(valid(step, -1))
        def _():
            rim_copies[n].wait_send()


def spread_kernel(grown_ref, out_ref):
    rhs, nx, ny, nz = out_ref.shape
    side = nx // 4
    for r in range(rhs):
        slices = [
            grown_ref[at * ny:(at + 1) * ny, r * nz:(r + 1) * nz] for at in range(side + 1)
        ]
        for x in range(nx):
            at, k = x // 4, x % 4
            if k == 0:
                out_ref[r, x] = slices[at]
            else:
                out_ref[r, x] = (1 - k / 4) * slices[at] + (k / 4) * slices[at + 1]


def per_device(peers, right_side, iterate, coefficient, ordering, leaf_inverse, leaf_first,
               leaf_second, leaf_top, first_inverse, first_second, first_top, second_inverse,
               second_top, top_inverse):
    rhs, nx, ny, nz = iterate.shape
    side = nx // 4
    slabs = side + 2
    pad_y = up_to(ny // 4, TILE)
    pad_z = LANES // rhs // 4 if nz // 4 <= LANES // rhs // 4 else LANES // rhs
    mats = [jnp.asarray(m, bf16) for m in constants(rhs, ny, nz, side, pad_y, pad_z)]
    flip = lambda m: jnp.swapaxes(m, -1, -2)
    flat = lambda m: m.reshape(m.shape[-2:])
    single_rows = lambda m: m.reshape(m.shape[-2], 1, m.shape[-1])
    rows = [single_rows(first_inverse), single_rows(second_inverse), top_inverse]
    spans = [m.shape[0] for m in rows]
    counts = [m.shape[-1] // s for m, s in zip(rows, spans)]
    seats = [up_to(s, 16) for s in spans]
    seats[0] = seats[1] = PITCH
    widths = [counts[0] * PITCH, up_to(counts[1] * PITCH, LANES), rows[2].shape[-1]]
    leaf = leaf_inverse.shape[-1]
    cells = ordering.shape[-1]
    at_first_level = up_to(leaf, 16)
    at_second = at_first_level + PITCH
    at_top = at_second + PITCH
    slots = up_to(at_top + spans[2], LANES)
    vmem = lambda *shape: pltpu.VMEM(shape, f32)
    split = lambda *shape: [pltpu.VMEM(shape, bf16)] * 2
    like = lambda m: pltpu.VMEM(m.shape, m.dtype)
    dma = lambda n: pltpu.SemaphoreType.DMA((n,))
    sizes = {
        "peers": peers, "pad_y": pad_y, "pad_z": pad_z, "spans": spans, "seats": seats,
        "widths": widths, "starts": (at_first_level, at_second, at_top),
    }
    matrices = (
        ordering.reshape(1, cells), single_rows(leaf_inverse),
        single_rows(flip(leaf_first)), single_rows(flip(leaf_second)), flat(flip(leaf_top)),
        single_rows(first_second), single_rows(first_top), single_rows(second_top),
    )
    operands = (right_side, iterate, coefficient, *matrices, *rows, *mats)
    edge_rows = up_to(slabs, TILE)
    face_rows = up_to(side, TILE)
    main = side * pad_y

    def share_shape(step):
        dx, dy, _ = step
        return (edge_rows if dy else (pad_y if dx else main), LANES)

    in_vmem = pl.BlockSpec(memory_space=pltpu.VMEM)
    anywhere = pl.BlockSpec(memory_space=pl.ANY)
    links = 2 * sum(seats)
    big_rows = LANES + 2 * PITCH
    grown = pl.pallas_call(
        functools.partial(kernel, sizes),
        out_shape=jax.ShapeDtypeStruct(((side + 1) * ny, rhs * nz), f32),
        in_specs=jax.tree.map(lambda _: anywhere, operands),
        out_specs=in_vmem,
        scratch_shapes=[
            like(right_side), like(iterate), like(coefficient), *[like(m) for m in matrices],
            [like(m) for m in rows],
            pltpu.VMEM(mats[0].shape[1:], bf16), like(mats[1]),
            pltpu.VMEM(mats[2].shape[1:], bf16), like(mats[3]), like(mats[4]),
            split(leaf, leaf),
            split(links, leaf),
            vmem(PITCH, 2 * seats[1]),
            vmem(2 * PITCH, 2 * seats[2]),
            [vmem(spans[level], widths[level]) for level in range(2)],
            split(2 * seats[0], widths[0]),
            split(2 * seats[1], widths[1]),
            split(big_rows, widths[2]),
            split(at_top, widths[0]),
            split(at_top, widths[1] + widths[0]),
            split(counts[0] * PITCH, widths[1]),
            vmem(2 * slabs * ny, rhs * nz),
            vmem(3, slabs * pad_y + 2 * edge_rows, LANES),
            [vmem(*share_shape(step)) for step in SHARES],
            [like(m) for m in rows],
            [vmem(n, rhs, LANES) for n in counts],
            [vmem(n, rhs, LANES) for n in counts],
            [vmem(n, rhs, LANES) for n in counts],
            vmem(rhs, widths[2]),
            vmem(rhs, widths[1] + widths[0]),
            vmem(rhs, slots),
            vmem(rhs, 2 * seats[2]),
            vmem(1, slots),
            vmem(rhs, slots),
            vmem(2, main + pad_y + 2 * face_rows, LANES),
            vmem(face_rows, LANES),
            [vmem(rhs, LANES) for _ in rows],
            vmem(PITCH, widths[1]),
            vmem(counts[0], PITCH, widths[1]),
            dma(2 * rhs + 24), dma(len(SHARES)), dma(len(SHARES)), dma(3), dma(3), dma(2),
            dma(3), dma(3), dma(3), dma(3), dma(len(RIMS)), dma(len(RIMS)),
        ],
        compiler_params=pltpu.CompilerParams(has_side_effects=True, collective_id=0),
    )(*operands)
    return pl.pallas_call(
        spread_kernel,
        out_shape=jax.ShapeDtypeStruct(iterate.shape, f32),
        in_specs=[in_vmem],
        out_specs=in_vmem,
    )(grown)


def solution(mesh):
    peers = dict(mesh.shape)
    return jax.shard_map(
        functools.partial(per_device, peers),
        mesh=mesh,
        in_specs=(
            P(None, "gx", "gy", "gz"),
            P(None, "gx", "gy", "gz"),
            P("gx", "gy", "gz"),
            P("gx", "gy", "gz", None),
            P("gx", "gy", "gz", None, None),
            P("gx", "gy", "gz", None, None),
            P("gx", "gy", "gz", None, None),
            P("gx", "gy", "gz", None, None),
            P("gx", "gy", "gz", None),
            P("gx", "gy", "gz", None, None),
            P("gx", "gy", "gz", None, None),
            P("gx", ("gy", "gz"), None),
            P("gx", "gy", "gz", None, None),
            P(("gx", "gy", "gz"), None),
        ),
        out_specs=P(None, "gx", "gy", "gz"),
        check_vma=False,
    )
```

time: 42.2 us -> 35.4 us (0.84)
  Pallas kernels: 42 us -> 35.3 us
    pallas_call x1, Pallas kernels: 39.8 us -> 33.1 us  [per_device(): pl.pallas_call(functools.partial(kernel, sizes), out_shape=jax.ShapeDtype...]
where the time goes in v1:
time: 35.4 us; the launch traced here: 35.3 us
  Pallas kernels  35.3 us (100%)
    pallas_call x1, Pallas kernels, per_device(): pl.pallas_call(functools.partial(kernel, sizes), out_shape=jax.ShapeDtype...  33.1 us
    pallas_call x1, Pallas kernels, per_device(): pl.pallas_call(spread_kernel, out_shape=jax.ShapeDtypeStruct(iterate.shap...  2.2 us

profile of v1, /device:TPU:0, one launch (start us, length us, event | category | flops | bytes accessed | tf_op | source)
XLA Modules:
  0.0 35.3 jit_solution(17581627932847961757)
XLA Ops:
  0.0 33.1 %shard_map.181.grown_ref = f32[168,96]{1,0:T(8,128)} custom-call(f32[4,24,24,24]{3,2,1,0:T(8,128)} %right_ref.1, f32[4,24,24,24]{3,2,1,0:T(8,128)} %u_ref.1, f32[24,24,24]{2,1,0:T(8,128)} %coef_ref.1, s32[1,216]{1,0:T(1,128)} %bitcast.29, f32[125,1,125]{2,1,0:T(1,128)} %bitcast.20, f32[50,1,125]{2,1,0:T(1,128)} %bitcast.24, f32[60,1,125]{2,1,0:T(1,128)} %bitcast.22, ...), custom_call_target="tpu_custom_call" | custom-call | tf_op jit(solution)/shard_map/pallas_call | solution.py:741
  33.1 2.2 %shard_map.182 = f32[4,24,24,24]{3,2,1,0:T(8,128)} custom-call(f32[168,96]{1,0:T(8,128)} %shard_map.181.grown_ref), custom_call_target="tpu_custom_call" | custom-call | tf_op jit(solution)/shard_map/pallas_call | solution.py:785

commit v2 on v1

--- a/solution.py
+++ b/solution.py
@@ -172,8 +172,8 @@
     fs_in, ft_in, st_in, rows_in, m_rows, m_lanes, m_beside, m_wide, m_tall,
     leaf_split, link_split, fs_seat, ftst_seat, row_seat, rows0, rows1, big, w0, zed, kay,
     packed, shares, share_in, prev, scatter_out, scatter_in, gather_in, top_all, val,
-    picked, slots, order_seat, ordered, rim, face, stage, k_own, k_all,
-    in_sem, share_send, share_recv, prev_send, prev_recv, k_sem, s_send, s_recv, g_send, g_recv,
+    picked, inner, slots, order_seat, ordered, rim, face, stage, k_own, k_all,
+    in_sem, ready, share_send, share_recv, prev_send, prev_recv, k_sem, s_send, s_recv, g_send, g_recv,
     r_send, r_recv,
 ):
     rhs, nx, ny, nz = u_in.shape
@@ -210,17 +210,24 @@
             at = me[a] + k
             turned[a].append(jnp.where(at >= peers[a], at - peers[a], at))
 
+    n_gx = peers["gx"]
+    far = [jnp.where(2 * me["gx"] < n_gx, n_gx - 1 - k, k) for k in range(n_gx)]
+
     def for_others(group, send):
         count = int(np.prod([peers[a] for a in group]))
         if count <= UNROLL:
             for steps in itertools.product(*[range(peers[a]) for a in group]):
-                if any(steps):
-                    target = dict(me)
-                    at = 0
-                    for a, k in zip(group, steps):
-                        target[a] = turned[a][k]
-                        at = at * peers[a] + turned[a][k]
+                target = dict(me)
+                at = 0
+                for a, k in zip(group, steps):
+                    target[a] = far[k] if a == "gx" else turned[a][k]
+                    at = at * peers[a] + target[a]
+                if any(steps[-2:]):
                     send(target, at)
+                elif len(steps) == 3:
+                    @pl.when(target["gx"] != me["gx"])
+                    def _():
+                        send(target, at)
         else:
             mine = place(group)
 
@@ -231,8 +238,19 @@
 
             lax.fori_loop(1, count, step, 0)
 
+    def valid(step, sign):
+        ok = None
+        for a, d in zip(AXES, step):
+            if d:
+                at = me[a] + sign * d
+                this = (at >= 0) & (at < peers[a])
+                ok = this if ok is None else ok & this
+        return ok
+
+    def toward(step, sign):
+        return {a: (me[a] + sign * d + peers[a]) % peers[a] for a, d in zip(AXES, step)}
+
     barrier = pltpu.get_barrier_semaphore()
-    everyone = counts[2]
 
     def greet(target, at):
         pl.semaphore_signal(barrier, inc=1, device_id=target, device_id_type=MESH)
@@ -251,6 +269,11 @@
     load("m_rows", mat_rows.at[at_y], m_rows)
     load("m_lanes", mat_lanes, m_lanes)
     load("m_beside", mat_beside.at[at_z], m_beside)
+    pack = rhs // 2
+
+    def slot(r):
+        return r % 2 * pack + r // 2
+
     row_sources = (rows_first, rows_second, rows_top)
     for level in range(3):
         load(("rows", level), row_sources[level], rows_in[level])
@@ -271,7 +294,39 @@
     for buffer in share_in:
         clear(buffer)
     clear(rim)
-    for_others(AXES, greet)
+    for_others(groups[1], greet)
+    for step in itertools.product((1, -1), SIDES, SIDES):
+        @pl.when(valid(step, 1))
+        def _():
+            greet(toward(step, 1), 0)
+
+    def beside(a):
+        return jnp.where(me[a] > 0, 1, 0) + jnp.where(me[a] < peers[a] - 1, 1, 0)
+
+    near_count = counts[1] - 1 + beside("gx") * (1 + beside("gy")) * (1 + beside("gz"))
+
+    def relay(step):
+        if step:
+            @pl.when(me["gx"] >= step)
+            def _():
+                pl.semaphore_wait(ready.at[0, step - 1], 1)
+
+            @pl.when(me["gx"] + step < n_gx)
+            def _():
+                pl.semaphore_wait(ready.at[1, step - 1], 1)
+
+        if step < n_gx - 1:
+            @pl.when((me["gx"] < n_gx - 1) & (me["gx"] >= step))
+            def _():
+                pl.semaphore_signal(
+                    ready.at[0, step], inc=1, device_id=toward((1, 0, 0), 1), device_id_type=MESH
+                )
+
+            @pl.when((me["gx"] > 0) & (me["gx"] + step < n_gx))
+            def _():
+                pl.semaphore_signal(
+                    ready.at[1, step], inc=1, device_id=toward((1, 0, 0), -1), device_id_type=MESH
+                )
 
     for level in range(3):
         @pl.when(me[shift_axis[level]] == 0)
@@ -321,21 +376,9 @@
     for t in range(3):
         shares[t] = c[:, t * LANES:(t + 1) * LANES]
 
-    def valid(step, sign):
-        ok = None
-        for a, d in zip(AXES, step):
-            if d:
-                at = me[a] + sign * d
-                this = (at >= 0) & (at < peers[a])
-                ok = this if ok is None else ok & this
-        return ok
-
-    def toward(step, sign):
-        return {a: (me[a] + sign * d + peers[a]) % peers[a] for a, d in zip(AXES, step)}
-
     for level in range(3):
         loads["rows", level].wait()
-    pl.semaphore_wait(barrier, everyone - 1)
+    pl.semaphore_wait(barrier, near_count)
 
     edge_rows = up_to(slabs, TILE)
     main = side * pad_y
@@ -373,6 +416,8 @@
         def _():
             copy.start()
 
+    relay(0)
+
     def keep(where, value, rows=None):
         high, low = halves(value)
         if rows is None:
@@ -455,6 +500,7 @@
             row_seat[level][:, d * PITCH:d * PITCH + span] = value[:, d * span:(d + 1) * span]
         return row_seat[level][...]
 
+    relay(1)
     links = dot_back(rows_of(leaf_in), link_split)
     wait_prev(0)
     own0 = seat_lanes(rows_of(rows_in[0]), 0)
@@ -463,11 +509,8 @@
     keep(rows0, seat_lanes(rows_of(prev[0]), 0), slice(seats[0], seats[0] + spans[0]))
     e0 = dot(links[:, :2 * seats[0]], rows0)
     keep(w0, -e0, slice(0, leaf))
-    wait_prev(1)
     own1 = seat_lanes(rows_of(rows_in[1]), 1)
     keep(rows1, own1, slice(0, spans[1]))
-    keep(rows1, seat_lanes(rows_of(prev[1]), 1), slice(seats[1], seats[1] + spans[1]))
-    k_own[...] = dot(fs_seat[...], rows1)
     mine0 = place(groups[0])
 
     def send_k(target, at):
@@ -477,28 +520,12 @@
             device_id=target, device_id_type=MESH,
         ).start()
 
-    for_others(groups[0], send_k)
-    k_all[mine0] = k_own[...]
-
     def all_slots(buffer, sem, count):
         return pltpu.make_async_copy(
             buffer.at[pl.ds(0, count - 1)], buffer.at[pl.ds(0, count - 1)], sem
         )
 
-    e1 = dot(links[:, 2 * seats[0]:2 * (seats[0] + seats[1])], rows1)
-    w1_value = jnp.concatenate([
-        -e1, jnp.zeros((at_second - leaf, e1.shape[1]), f32), own1,
-        jnp.zeros((at_top - at_second - spans[1], e1.shape[1]), f32),
-    ], 0)
-    all_slots(k_all, k_sem.at[1], n_gz).wait()
-    keep(kay, k_all[...].reshape(n_gz * PITCH, k_own.shape[1]))
-    w0_value = w0[0][...].astype(f32) + w0[1][...].astype(f32)
-    gap_width = widths[1]
-    zed_value = w1_value - dot(w0_value, kay)
-    high, low = halves(zed_value)
-    zed[0][:, :gap_width], zed[1][:, :gap_width] = high, low
-    zed[0][:, gap_width:], zed[1][:, gap_width:] = w0[0][...], w0[1][...]
-
+    relay(2)
     received = {}
     for n, step in enumerate(SHARES):
         @pl.when(valid(step, -1))
@@ -521,13 +548,18 @@
     coarse = jnp.concatenate(pieces, 0)
     for r in range(rhs):
         spread = dot_exact(coarse, lane_hot(r))
-        picked[r:r + 1, :] = jnp.sum(spread * pick_hot, axis=0, keepdims=True)
+        picked[slot(r):slot(r) + 1, :] = jnp.sum(spread * pick_hot, axis=0, keepdims=True)
 
     def scatter(level, terms, pitch, lane):
         span, group = spans[level], groups[level]
         out, into = scatter_out[level], scatter_in[level]
         for d in range(counts[level]):
-            out[d, :, lane:lane + span] = terms[:, d * pitch:d * pitch + span]
+            part = terms[:, d * pitch:d * pitch + span]
+            if level == 2:
+                out[d, :, :span] = part[:pack]
+                out[d, :, LANES // 2:LANES // 2 + span] = part[pack:]
+            else:
+                out[d, :, lane:lane + span] = part
         mine = place(group)
 
         def send(target, d):
@@ -566,34 +598,58 @@
         all_slots(into, g_recv.at[level], counts[level]).wait()
         return into
 
-    below_top = picked[:, :at_top]
-    scatter(1, dot(below_top, (zed[0][:, :gap_width], zed[1][:, :gap_width])), PITCH, 0)
-    scatter(0, dot(below_top, w0), PITCH, PITCH)
+    scatter(0, dot(picked[:, :at_top], w0), PITCH, PITCH)
+    leaf_rhs = picked[:, :leaf]
+    lows = dot(leaf_rhs, halves(links[:, 2 * seats[0]:]))
+    pair1, pair2 = 2 * seats[1], 2 * seats[2]
+    inner[...] = -lows[:, :pair1]
+    inner[:, :spans[1]] = picked[:, at_second:at_second + spans[1]] - lows[:, :spans[1]]
+    slots[...] = -lows[:, pair1:]
+    slots[:, :spans[2]] = picked[:, at_top:at_top + spans[2]] - lows[:, pair1:pair1 + spans[2]]
+    wait_prev(1)
+    keep(rows1, seat_lanes(rows_of(prev[1]), 1), slice(seats[1], seats[1] + spans[1]))
+    k_own[...] = dot(fs_seat[...], rows1)
+    base1 = dot(inner[...], rows1)
+    k_halves = halves(k_own[...])
+    first_own = scatter_end(0)
+    scatter(1, base1 - dot(first_own[:, PITCH:2 * PITCH], k_halves), PITCH, 0)
+    for_others(groups[0], send_k)
+    k_all[mine0] = k_own[...]
 
     wait_prev(2)
     keep(big, rows_of(rows_in[2]), slice(0, spans[2]))
     keep(big, rows_of(prev[2]), slice(seats[2], seats[2] + spans[2]))
-    pair2 = 2 * seats[2]
     rows2 = (big[0].at[pl.ds(0, pair2)], big[1].at[pl.ds(0, pair2)])
     queue = slice(LANES, LANES + 2 * PITCH)
     keep(big, dot(ftst_seat[...], rows2), queue)
-    leaf_rhs = picked[:, :leaf]
-    tops = dot(leaf_rhs, halves(links[:, 2 * (seats[0] + seats[1]):]))
-    slots[...] = -tops
-    slots[:, :spans[2]] = picked[:, at_top:at_top + spans[2]] - tops[:, :spans[2]]
     base2 = dot(slots[...], rows2)
-    first_own = scatter_end(0)
     queue_rows = (big[0].at[queue], big[1].at[queue])
     base2 = base2 - dot(first_own[:, :2 * PITCH], queue_rows)
     leaf_solved = dot(leaf_rhs, leaf_split)
     second_own = scatter_end(1)
+    for step in range(3, n_gx):
+        relay(step)
     scatter(2, base2 - dot(second_own[:, :2 * PITCH], queue_rows), spans[2], 0)
     both_own = (first_own + second_own)[:, :2 * PITCH]
+    e1 = dot(links[:, 2 * seats[0]:2 * (seats[0] + seats[1])], rows1)
+    w1_value = jnp.concatenate([
+        -e1, jnp.zeros((at_second - leaf, e1.shape[1]), f32), own1,
+        jnp.zeros((at_top - at_second - spans[1], e1.shape[1]), f32),
+    ], 0)
+    all_slots(k_all, k_sem.at[1], n_gz).wait()
+    keep(kay, k_all[...].reshape(n_gz * PITCH, k_own.shape[1]))
+    w0_value = w0[0][...].astype(f32) + w0[1][...].astype(f32)
+    gap_width = widths[1]
+    high, low = halves(w1_value - dot(w0_value, kay))
+    zed[0][:, :gap_width], zed[1][:, :gap_width] = high, low
+    zed[0][:, gap_width:], zed[1][:, gap_width:] = w0[0][...], w0[1][...]
     top_own = scatter_end(2)
     gather(2, top_own)
     into = gather_end(2)
     for d in range(counts[2]):
-        top_all[:, d * spans[2]:(d + 1) * spans[2]] = into[d, :, :spans[2]]
+        at = slice(d * spans[2], (d + 1) * spans[2])
+        top_all[:pack, at] = into[d, :, :spans[2]]
+        top_all[pack:, at] = into[d, :, LANES // 2:LANES // 2 + spans[2]]
     solved = dot_back(top_all[...], big)
     gather(1, jnp.concatenate([
         both_own - solved[:, LANES:LANES + 2 * PITCH], jnp.zeros((rhs, LANES - 2 * PITCH), f32)
@@ -629,7 +685,7 @@
 
     cells_back = None
     for r in range(rhs):
-        term = dot_exact(back_hot * ordered[r:r + 1, :], lane_hot(r), single_back)
+        term = dot_exact(back_hot * ordered[slot(r):slot(r) + 1, :], lane_hot(r), single_back)
         cells_back = term if cells_back is None else cells_back + term
     rim[0, 0:main] = cells_back[:main]
     face[...] = cells_back[main:]
@@ -673,9 +729,10 @@
             rim_copies[n].wait_send()
 
 
-def spread_kernel(grown_ref, out_ref):
+def spread_kernel(grown_ref, out_ref, held, sem):
     rhs, nx, ny, nz = out_ref.shape
     side = nx // 4
+    copies = []
     for r in range(rhs):
         slices = [
             grown_ref[at * ny:(at + 1) * ny, r * nz:(r + 1) * nz] for at in range(side + 1)
@@ -683,9 +740,14 @@
         for x in range(nx):
             at, k = x // 4, x % 4
             if k == 0:
-                out_ref[r, x] = slices[at]
+                held[r, x] = slices[at]
             else:
-                out_ref[r, x] = (1 - k / 4) * slices[at] + (k / 4) * slices[at + 1]
+                held[r, x] = (1 - k / 4) * slices[at] + (k / 4) * slices[at + 1]
+        copy = pltpu.make_async_copy(held.at[r], out_ref.at[r], sem.at[r])
+        copy.start()
+        copies.append(copy)
+    for copy in copies:
+        copy.wait()
 
 
 def per_device(peers, right_side, iterate, coefficient, ordering, leaf_inverse, leaf_first,
@@ -737,10 +799,11 @@
     in_vmem = pl.BlockSpec(memory_space=pltpu.VMEM)
     anywhere = pl.BlockSpec(memory_space=pl.ANY)
     links = 2 * sum(seats)
+    packs = (rhs, rhs, rhs // 2)
     big_rows = LANES + 2 * PITCH
     grown = pl.pallas_call(
         functools.partial(kernel, sizes),
-        out_shape=jax.ShapeDtypeStruct(((side + 1) * ny, rhs * nz), f32),
+        out_shape=pltpu.VMEM(((side + 1) * ny, rhs * nz), f32),
         in_specs=jax.tree.map(lambda _: anywhere, operands),
         out_specs=in_vmem,
         scratch_shapes=[
@@ -763,21 +826,22 @@
             vmem(3, slabs * pad_y + 2 * edge_rows, LANES),
             [vmem(*share_shape(step)) for step in SHARES],
             [like(m) for m in rows],
-            [vmem(n, rhs, LANES) for n in counts],
-            [vmem(n, rhs, LANES) for n in counts],
-            [vmem(n, rhs, LANES) for n in counts],
+            [vmem(n, p, LANES) for n, p in zip(counts, packs)],
+            [vmem(n, p, LANES) for n, p in zip(counts, packs)],
+            [vmem(n, p, LANES) for n, p in zip(counts, packs)],
             vmem(rhs, widths[2]),
             vmem(rhs, widths[1] + widths[0]),
             vmem(rhs, slots),
+            vmem(rhs, 2 * seats[1]),
             vmem(rhs, 2 * seats[2]),
             vmem(1, slots),
             vmem(rhs, slots),
             vmem(2, main + pad_y + 2 * face_rows, LANES),
             vmem(face_rows, LANES),
-            [vmem(rhs, LANES) for _ in rows],
+            [vmem(p, LANES) for p in packs],
             vmem(PITCH, widths[1]),
             vmem(counts[0], PITCH, widths[1]),
-            dma(2 * rhs + 24), dma(len(SHARES)), dma(len(SHARES)), dma(3), dma(3), dma(2),
+            dma(2 * rhs + 24), pltpu.SemaphoreType.REGULAR((2, max(peers["gx"] - 1, 1))), dma(len(SHARES)), dma(len(SHARES)), dma(3), dma(3), dma(2),
             dma(3), dma(3), dma(3), dma(3), dma(len(RIMS)), dma(len(RIMS)),
         ],
         compiler_params=pltpu.CompilerParams(has_side_effects=True, collective_id=0),
@@ -786,8 +850,9 @@
         spread_kernel,
         out_shape=jax.ShapeDtypeStruct(iterate.shape, f32),
         in_specs=[in_vmem],
-        out_specs=in_vmem,
-    )(grown)
+        out_specs=anywhere,
+        scratch_shapes=[like(iterate), dma(rhs)],
+    )(pltpu.with_memory_space_constraint(grown, pltpu.VMEM))
 
 
 def solution(mesh):

time: 35.4 us -> 32.4 us (0.915)
  Pallas kernels: 35.3 us -> 32.2 us
    pallas_call x1, Pallas kernels: 33.1 us -> 31.1 us  [per_device(): pl.pallas_call(functools.partial(kernel, sizes), out_shape=pltpu.VMEM(((s...]
    pallas_call x1, Pallas kernels: 2.2 us -> 1.09 us  [per_device(): pl.pallas_call(spread_kernel, out_shape=jax.ShapeDtypeStruct(iterate.shap...]
where the time goes in v2:
time: 32.4 us; the launch traced here: 32.2 us
  Pallas kernels  32.2 us (99%)
    pallas_call x1, Pallas kernels, per_device(): pl.pallas_call(functools.partial(kernel, sizes), out_shape=pltpu.VMEM(((s...  31.1 us
    pallas_call x1, Pallas kernels, per_device(): pl.pallas_call(spread_kernel, out_shape=jax.ShapeDtypeStruct(iterate.shap...  1.09 us

profile of v2, /device:TPU:0, one launch (start us, length us, event | category | flops | bytes accessed | tf_op | source)
XLA Modules:
  0.0 32.2 jit_solution(2841377988452538948)
XLA Ops:
  0.0 31.1 %shard_map.181.grown_ref = f32[168,96]{1,0:T(8,128)S(1)} custom-call(f32[4,24,24,24]{3,2,1,0:T(8,128)} %right_ref.1, f32[4,24,24,24]{3,2,1,0:T(8,128)} %u_ref.1, f32[24,24,24]{2,1,0:T(8,128)} %coef_ref.1, s32[1,216]{1,0:T(1,128)} %bitcast.29, f32[125,1,125]{2,1,0:T(1,128)} %bitcast.20, f32[50,1,125]{2,1,0:T(1,128)} %bitcast.24, f32[60,1,125]{2,1,0:T(1,128)} %bitcast.22, ...), custom_call_target="tpu_custom_call" | custom-call | tf_op jit(solution)/shard_map/pallas_call | solution.py:804
  31.1 1.1 %shard_map.182 = f32[4,24,24,24]{3,2,1,0:T(8,128)} custom-call(f32[168,96]{1,0:T(8,128)S(1)} %shard_map.181.grown_ref), custom_call_target="tpu_custom_call" | custom-call | tf_op jit(solution)/shard_map/pallas_call | solution.py:849

commit v3 on v2

--- a/solution.py
+++ b/solution.py
@@ -26,7 +26,9 @@
     for k in SIDES
     if (i, j, k) != (0, 0, 0) and (i, j, k).count(-1) <= 1
 ]
+SHARES.sort(key=lambda step: -2 * abs(step[1]) - abs(step[0]))
 RIMS = [(i, j, k) for i in (0, 1) for j in (0, 1) for k in (0, 1) if (i, j, k) != (0, 0, 0)]
+RIMS.sort(key=lambda step: -2 * step[1] - step[0])
 
 
 def up_to(n, unit):
@@ -166,21 +168,22 @@
     sizes,
     right_ref, u_ref, coef_ref, order_ref, leaf_ref, first_ref, second_ref, top_ref,
     fs_ref, ft_ref, st_ref, rows_first, rows_second, rows_top,
-    mat_rows, mat_lanes, mat_beside, mat_wide, mat_tall,
+    mat_rows, mat_lanes, mat_beside, mat_wide, mat_tall, blank,
     out_ref,
     right_in, u_in, coef_in, order_in, leaf_in, first_in, second_in, top_in,
     fs_in, ft_in, st_in, rows_in, m_rows, m_lanes, m_beside, m_wide, m_tall,
-    leaf_split, link_split, fs_seat, ftst_seat, row_seat, rows0, rows1, big, w0, zed, kay,
+    leaf_split, link_split, fs_seat, ftst_seat, row_seat, rows0, rows1, big, w0, w1, zed, kay,
     packed, shares, share_in, prev, scatter_out, scatter_in, gather_in, top_all, val,
-    picked, inner, slots, order_seat, ordered, rim, face, stage, k_own, k_all,
-    in_sem, ready, share_send, share_recv, prev_send, prev_recv, k_sem, s_send, s_recv, g_send, g_recv,
-    r_send, r_recv,
+    picked, slots, order_seat, ordered, rim, face, stage, k_own, k_all,
+    in_sem, ready, share_recv, rim_recv, prev_recv, k_sem, s_recv, g_recv,
 ):
     rhs, nx, ny, nz = u_in.shape
     side = nx // 4
     side_y, side_z = ny // 4, nz // 4
     slabs = side + 2
     pad_y, pad_z = sizes["pad_y"], sizes["pad_z"]
+    edge_rows = up_to(slabs, TILE)
+    main = side * pad_y
     spans, seats, widths = sizes["spans"], sizes["seats"], sizes["widths"]
     leaf = leaf_in.shape[0]
     at_first_level, at_second, at_top = sizes["starts"]
@@ -208,7 +211,10 @@
     for a in AXES:
         for k in range(1, peers[a]):
             at = me[a] + k
-            turned[a].append(jnp.where(at >= peers[a], at - peers[a], at))
+            if peers[a] & (peers[a] - 1):
+                turned[a].append(jnp.where(at >= peers[a], at - peers[a], at))
+            else:
+                turned[a].append(me[a] ^ k)
 
     n_gx = peers["gx"]
     far = [jnp.where(2 * me["gx"] < n_gx, n_gx - 1 - k, k) for k in range(n_gx)]
@@ -220,7 +226,7 @@
                 target = dict(me)
                 at = 0
                 for a, k in zip(group, steps):
-                    target[a] = far[k] if a == "gx" else turned[a][k]
+                    target[a] = far[k] if a == "gx" else turned[a][-k]
                     at = at * peers[a] + target[a]
                 if any(steps[-2:]):
                     send(target, at)
@@ -288,12 +294,36 @@
     load("m_wide", mat_wide, m_wide)
     load("m_tall", mat_tall, m_tall)
 
+    share_at = [0]
+    for step in SHARES:
+        dx, dy, dz = step
+        share_at.append(share_at[-1] + (edge_rows if dy else (pad_y if dx else main)))
+    for n, step in enumerate(SHARES):
+        @pl.when(jnp.logical_not(valid(step, -1)))
+        def _():
+            part = pl.ds(share_at[n], share_at[n + 1] - share_at[n])
+            pltpu.make_async_copy(
+                blank.at[pl.ds(0, share_at[n + 1] - share_at[n])], share_in.at[part], share_recv
+            ).start()
+    face_rows = face.shape[0]
+
+    def rim_place(step):
+        dx, dy, dz = step
+        if dy:
+            return face_rows, main + pad_y + (face_rows if dx else 0)
+        return (pad_y, main) if dx else (main, 0)
+
+    for n, step in enumerate(RIMS):
+        @pl.when(jnp.logical_not(valid(step, 1)))
+        def _():
+            rows, at = rim_place(step)
+            pltpu.make_async_copy(
+                blank.at[pl.ds(0, rows)], rim.at[step[2], pl.ds(at, rows)], rim_recv
+            ).start()
+
     def clear(ref):
         ref[...] = jnp.zeros(ref.shape, ref.dtype)
 
-    for buffer in share_in:
-        clear(buffer)
-    clear(rim)
     for_others(groups[1], greet)
     for step in itertools.product((1, -1), SIDES, SIDES):
         @pl.when(valid(step, 1))
@@ -376,12 +406,11 @@
     for t in range(3):
         shares[t] = c[:, t * LANES:(t + 1) * LANES]
 
-    for level in range(3):
-        loads["rows", level].wait()
+    for name in loads:
+        if name not in ("coef", "m_rows", "m_lanes", "m_beside") and name[0] not in ("u", "right"):
+            loads[name].wait()
     pl.semaphore_wait(barrier, near_count)
 
-    edge_rows = up_to(slabs, TILE)
-    main = side * pad_y
     share_copies = []
     for n, step in enumerate(SHARES):
         dx, dy, dz = step
@@ -390,8 +419,9 @@
         else:
             cut = pl.ds(slabs * pad_y + (edge_rows if dy < 0 else 0), edge_rows)
         copy = pltpu.make_async_remote_copy(
-            src_ref=shares.at[SIDES.index(dz), cut], dst_ref=share_in[n],
-            send_sem=share_send.at[n], recv_sem=share_recv.at[n],
+            src_ref=shares.at[SIDES.index(dz), cut],
+            dst_ref=share_in.at[pl.ds(share_at[n], share_at[n + 1] - share_at[n])],
+            send_sem=in_sem.at[n], recv_sem=share_recv,
             device_id=toward(step, 1), device_id_type=MESH,
         )
         share_copies.append(copy)
@@ -407,7 +437,7 @@
         target[axis] = (me[axis] + 1) % peers[axis]
         copy = pltpu.make_async_remote_copy(
             src_ref=rows_in[level], dst_ref=prev[level],
-            send_sem=prev_send.at[level], recv_sem=prev_recv.at[level],
+            send_sem=in_sem.at[len(SHARES) + level], recv_sem=prev_recv.at[level],
             device_id=target, device_id_type=MESH,
         )
         prev_copies.append(copy)
@@ -429,11 +459,9 @@
     def rows_of(raw):
         return raw[:, 0, :] if len(raw.shape) == 3 else raw[...]
 
-    for name in ("leaf", "first", "second", "top", "fs", "ft", "st", "order"):
-        loads[name].wait()
     keep(leaf_split, rows_of(leaf_in))
     link_at = [0, 2 * seats[0], 2 * (seats[0] + seats[1])]
-    for pair in (link_split, rows0, rows1, big, w0):
+    for pair in (link_split, rows0, rows1, big, w0, w1):
         for part in pair:
             clear(part)
     for level, raw in enumerate((first_in, second_in, top_in)):
@@ -480,7 +508,6 @@
         (near & (second == 0)).astype(f32),
         (near & (second == side_y - 1)).astype(f32),
     ], 0)
-    face_rows = face.shape[0]
     face_hot = ((row_iota(face_rows) == first) & (second == 0)).astype(f32)
     back_hot = jnp.concatenate([main_hot, face_hot], 0)
     lane_id = lax.broadcasted_iota(jnp.int32, (LANES, cells), 0).astype(f32)
@@ -516,9 +543,15 @@
     def send_k(target, at):
         pltpu.make_async_remote_copy(
             src_ref=k_own, dst_ref=k_all.at[mine0],
-            send_sem=k_sem.at[0], recv_sem=k_sem.at[1],
+            send_sem=in_sem.at[len(SHARES) + 3], recv_sem=k_sem.at[0],
             device_id=target, device_id_type=MESH,
         ).start()
+
+    def s_send(level):
+        return in_sem.at[len(SHARES) + 4 + level]
+
+    def g_send(level):
+        return in_sem.at[len(SHARES) + 6 + level]
 
     def all_slots(buffer, sem, count):
         return pltpu.make_async_copy(
@@ -526,14 +559,22 @@
         )
 
     relay(2)
+    wait_prev(1)
+    keep(rows1, seat_lanes(rows_of(prev[1]), 1), slice(seats[1], seats[1] + spans[1]))
+    k_own[...] = dot(fs_seat[...], rows1)
+    for_others(groups[0], send_k)
+    k_all[mine0] = k_own[...]
+    e1 = dot(links[:, 2 * seats[0]:2 * (seats[0] + seats[1])], rows1)
+    w1_value = jnp.concatenate([
+        -e1, jnp.zeros((at_second - leaf, e1.shape[1]), f32), own1,
+        jnp.zeros((at_top - at_second - spans[1], e1.shape[1]), f32),
+    ], 0)
+    keep(w1, w1_value)
     received = {}
+    pltpu.make_async_copy(share_in, share_in, share_recv).wait()
     for n, step in enumerate(SHARES):
-        @pl.when(valid(step, -1))
-        def _():
-            share_copies[n].wait_recv()
-    for n, step in enumerate(SHARES):
-        dx, dy, dz = step
-        received[dx, dy] = received[dx, dy] + share_in[n][...] if (dx, dy) in received else share_in[n][...]
+        part = share_in[share_at[n]:share_at[n + 1]]
+        received[step[:2]] = received[step[:2]] + part if step[:2] in received else part
 
     total = shares[0, pad_y:pad_y + main] + received[0, 0]
     pieces = [total[:pad_y] + received[1, 0], total[pad_y:main - pad_y], total[main - pad_y:] + received[-1, 0]]
@@ -565,7 +606,7 @@
         def send(target, d):
             pltpu.make_async_remote_copy(
                 src_ref=out.at[d], dst_ref=into.at[mine],
-                send_sem=s_send.at[level], recv_sem=s_recv.at[level],
+                send_sem=s_send(level), recv_sem=s_recv.at[level],
                 device_id=target, device_id_type=MESH,
             ).start()
 
@@ -586,7 +627,7 @@
         def send(target, d):
             pltpu.make_async_remote_copy(
                 src_ref=own, dst_ref=into.at[mine],
-                send_sem=g_send.at[level], recv_sem=g_recv.at[level],
+                send_sem=g_send(level), recv_sem=g_recv.at[level - 1],
                 device_id=target, device_id_type=MESH,
             ).start()
 
@@ -595,26 +636,20 @@
 
     def gather_end(level):
         into = gather_in[level]
-        all_slots(into, g_recv.at[level], counts[level]).wait()
+        all_slots(into, g_recv.at[level - 1], counts[level]).wait()
         return into
 
-    scatter(0, dot(picked[:, :at_top], w0), PITCH, PITCH)
+    terms0 = dot(picked[:, :at_top], w0)
+    base1 = dot(picked[:, :at_top], w1)
+    all_slots(k_all, k_sem.at[0], n_gz).wait()
+    keep(kay, k_all[...].reshape(n_gz * PITCH, k_own.shape[1]))
+    scatter(1, base1 - dot(terms0, kay), PITCH, 0)
+    scatter(0, terms0, PITCH, PITCH)
     leaf_rhs = picked[:, :leaf]
-    lows = dot(leaf_rhs, halves(links[:, 2 * seats[0]:]))
-    pair1, pair2 = 2 * seats[1], 2 * seats[2]
-    inner[...] = -lows[:, :pair1]
-    inner[:, :spans[1]] = picked[:, at_second:at_second + spans[1]] - lows[:, :spans[1]]
-    slots[...] = -lows[:, pair1:]
-    slots[:, :spans[2]] = picked[:, at_top:at_top + spans[2]] - lows[:, pair1:pair1 + spans[2]]
-    wait_prev(1)
-    keep(rows1, seat_lanes(rows_of(prev[1]), 1), slice(seats[1], seats[1] + spans[1]))
-    k_own[...] = dot(fs_seat[...], rows1)
-    base1 = dot(inner[...], rows1)
-    k_halves = halves(k_own[...])
-    first_own = scatter_end(0)
-    scatter(1, base1 - dot(first_own[:, PITCH:2 * PITCH], k_halves), PITCH, 0)
-    for_others(groups[0], send_k)
-    k_all[mine0] = k_own[...]
+    lows = dot(leaf_rhs, halves(links[:, 2 * (seats[0] + seats[1]):]))
+    pair2 = 2 * seats[2]
+    slots[...] = -lows
+    slots[:, :spans[2]] = picked[:, at_top:at_top + spans[2]] - lows[:, :spans[2]]
 
     wait_prev(2)
     keep(big, rows_of(rows_in[2]), slice(0, spans[2]))
@@ -623,6 +658,7 @@
     queue = slice(LANES, LANES + 2 * PITCH)
     keep(big, dot(ftst_seat[...], rows2), queue)
     base2 = dot(slots[...], rows2)
+    first_own = scatter_end(0)
     queue_rows = (big[0].at[queue], big[1].at[queue])
     base2 = base2 - dot(first_own[:, :2 * PITCH], queue_rows)
     leaf_solved = dot(leaf_rhs, leaf_split)
@@ -631,13 +667,6 @@
         relay(step)
     scatter(2, base2 - dot(second_own[:, :2 * PITCH], queue_rows), spans[2], 0)
     both_own = (first_own + second_own)[:, :2 * PITCH]
-    e1 = dot(links[:, 2 * seats[0]:2 * (seats[0] + seats[1])], rows1)
-    w1_value = jnp.concatenate([
-        -e1, jnp.zeros((at_second - leaf, e1.shape[1]), f32), own1,
-        jnp.zeros((at_top - at_second - spans[1], e1.shape[1]), f32),
-    ], 0)
-    all_slots(k_all, k_sem.at[1], n_gz).wait()
-    keep(kay, k_all[...].reshape(n_gz * PITCH, k_own.shape[1]))
     w0_value = w0[0][...].astype(f32) + w0[1][...].astype(f32)
     gap_width = widths[1]
     high, low = halves(w1_value - dot(w0_value, kay))
@@ -662,9 +691,9 @@
         def _():
             prev_copies[level].wait_send()
 
-        all_slots(scatter_out[level], s_send.at[level], counts[level]).wait()
-    all_slots(k_all, k_sem.at[0], n_gz).wait()
-    all_slots(gather_in[2], g_send.at[2], counts[2]).wait()
+        all_slots(scatter_out[level], s_send(level), counts[level]).wait()
+    all_slots(k_all, in_sem.at[len(SHARES) + 3], n_gz).wait()
+    all_slots(gather_in[2], g_send(2), counts[2]).wait()
     for n, step in enumerate(SHARES):
         @pl.when(valid(step, 1))
         def _():
@@ -693,16 +722,11 @@
     rim_copies = []
     for n, step in enumerate(RIMS):
         dx, dy, dz = step
-        if dy:
-            source, at = face, main + pad_y + (face_rows if dx else 0)
-        elif dx:
-            source, at = rim.at[0, pl.ds(0, pad_y)], main
-        else:
-            source, at = rim.at[0, pl.ds(0, main)], 0
-        rows = face_rows if dy else (pad_y if dx else main)
+        rows, at = rim_place(step)
         copy = pltpu.make_async_remote_copy(
-            src_ref=source, dst_ref=rim.at[dz, pl.ds(at, rows)],
-            send_sem=r_send.at[n], recv_sem=r_recv.at[n],
+            src_ref=face if dy else rim.at[0, pl.ds(0, rows)],
+            dst_ref=rim.at[dz, pl.ds(at, rows)],
+            send_sem=in_sem.at[n], recv_sem=rim_recv,
             device_id=toward(step, -1), device_id_type=MESH,
         )
         rim_copies.append(copy)
@@ -711,13 +735,9 @@
         def _():
             copy.start()
 
-    loads["m_wide"].wait()
-    loads["m_tall"].wait()
-    all_slots(gather_in[1], g_send.at[1], counts[1]).wait()
-    for n, step in enumerate(RIMS):
-        @pl.when(valid(step, 1))
-        def _():
-            rim_copies[n].wait_recv()
+    all_slots(gather_in[1], g_send(1), counts[1]).wait()
+    arrived = share_in.at[pl.ds(0, 2 * rim.shape[1] - main)]
+    pltpu.make_async_copy(arrived, arrived, rim_recv).wait()
 
     wide = dot_exact(jnp.concatenate([rim[0], rim[1]], 1), m_wide[...])
     high, low = halves(wide)
@@ -787,10 +807,12 @@
         single_rows(flip(leaf_first)), single_rows(flip(leaf_second)), flat(flip(leaf_top)),
         single_rows(first_second), single_rows(first_top), single_rows(second_top),
     )
-    operands = (right_side, iterate, coefficient, *matrices, *rows, *mats)
     edge_rows = up_to(slabs, TILE)
     face_rows = up_to(side, TILE)
     main = side * pad_y
+    blank = np.zeros((main + TILE, LANES), np.float32)
+    blank[main:] = 1.0
+    operands = (right_side, iterate, coefficient, *matrices, *rows, *mats, jnp.asarray(blank))
 
     def share_shape(step):
         dx, dy, _ = step
@@ -820,11 +842,12 @@
             split(2 * seats[1], widths[1]),
             split(big_rows, widths[2]),
             split(at_top, widths[0]),
+            split(at_top, widths[1]),
             split(at_top, widths[1] + widths[0]),
             split(counts[0] * PITCH, widths[1]),
             vmem(2 * slabs * ny, rhs * nz),
             vmem(3, slabs * pad_y + 2 * edge_rows, LANES),
-            [vmem(*share_shape(step)) for step in SHARES],
+            vmem(sum(share_shape(step)[0] for step in SHARES), LANES),
             [like(m) for m in rows],
             [vmem(n, p, LANES) for n, p in zip(counts, packs)],
             [vmem(n, p, LANES) for n, p in zip(counts, packs)],
@@ -832,7 +855,6 @@
             vmem(rhs, widths[2]),
             vmem(rhs, widths[1] + widths[0]),
             vmem(rhs, slots),
-            vmem(rhs, 2 * seats[1]),
             vmem(rhs, 2 * seats[2]),
             vmem(1, slots),
             vmem(rhs, slots),
@@ -841,8 +863,9 @@
             [vmem(p, LANES) for p in packs],
             vmem(PITCH, widths[1]),
             vmem(counts[0], PITCH, widths[1]),
-            dma(2 * rhs + 24), pltpu.SemaphoreType.REGULAR((2, max(peers["gx"] - 1, 1))), dma(len(SHARES)), dma(len(SHARES)), dma(3), dma(3), dma(2),
-            dma(3), dma(3), dma(3), dma(3), dma(len(RIMS)), dma(len(RIMS)),
+            dma(max(len(SHARES) + 9, 2 * rhs + len(operands) - 3)),
+            pltpu.SemaphoreType.REGULAR((2, max(peers["gx"] - 1, 1))),
+            pltpu.SemaphoreType.DMA, pltpu.SemaphoreType.DMA, dma(3), dma(1), dma(3), dma(2),
         ],
         compiler_params=pltpu.CompilerParams(has_side_effects=True, collective_id=0),
     )(*operands)

time: 32.4 us -> 30.6 us (0.944)
  Pallas kernels: 32.2 us -> 30.4 us
    pallas_call x1, Pallas kernels: 31.1 us -> 29.3 us  [per_device(): pl.pallas_call(functools.partial(kernel, sizes), out_shape=pltpu.VMEM(((s...]
where the time goes in v3:
time: 30.6 us; the launch traced here: 30.4 us
  Pallas kernels  30.4 us (99%)
    pallas_call x1, Pallas kernels, per_device(): pl.pallas_call(functools.partial(kernel, sizes), out_shape=pltpu.VMEM(((s...  29.3 us
    pallas_call x1, Pallas kernels, per_device(): pl.pallas_call(spread_kernel, out_shape=jax.ShapeDtypeStruct(iterate.shap...  1.09 us

profile of v3, /device:TPU:0, one launch (start us, length us, event | category | flops | bytes accessed | tf_op | source)
XLA Modules:
  0.0 30.4 jit_solution(12264155380125588006)
XLA Ops:
  0.0 29.3 %shard_map.190.grown_ref = f32[168,96]{1,0:T(8,128)S(1)} custom-call(f32[4,24,24,24]{3,2,1,0:T(8,128)} %right_ref.1, f32[4,24,24,24]{3,2,1,0:T(8,128)} %u_ref.1, f32[24,24,24]{2,1,0:T(8,128)} %coef_ref.1, s32[1,216]{1,0:T(1,128)} %bitcast.29, f32[125,1,125]{2,1,0:T(1,128)} %bitcast.20, f32[50,1,125]{2,1,0:T(1,128)} %bitcast.24, f32[60,1,125]{2,1,0:T(1,128)} %bitcast.22, ...), custom_call_target="tpu_custom_call" | custom-call | tf_op jit(solution)/shard_map/pallas_call | solution.py:826
  29.4 1.1 %shard_map.191 = f32[4,24,24,24]{3,2,1,0:T(8,128)} custom-call(f32[168,96]{1,0:T(8,128)S(1)} %shard_map.190.grown_ref), custom_call_target="tpu_custom_call" | custom-call | tf_op jit(solution)/shard_map/pallas_call | solution.py:872

commit v4 on v3

--- a/solution.py
+++ b/solution.py
@@ -116,6 +116,25 @@
     return out
 
 
+def face_cuts(side, side_y, side_z):
+    faces = [side_y * side_z, side * side_z, side * side_y, side_y, side]
+    starts = [0]
+    for n in faces:
+        starts.append(starts[-1] + up_to(n, 16))
+    source = {
+        (1, 0, 0): (0, 0), (0, 1, 0): (1, 1), (0, 0, 1): (2, 2), (1, 1, 0): (0, None),
+        (1, 0, 1): (3, 3), (0, 1, 1): (4, 4), (1, 1, 1): (0, None),
+    }
+    cuts, at = {"rows": starts[-1], "starts": starts}, 0
+    for step in RIMS:
+        face, size = source[step]
+        rows = up_to(side_z if size is None else faces[size], TILE)
+        cuts[step] = (starts[face], rows, at)
+        at += up_to(rows, 16)
+    cuts["end"] = at
+    return cuts
+
+
 def constants(rhs, ny, nz, side, pad_y, pad_z):
     slabs = side + 2
     edge_rows = up_to(slabs, TILE)
@@ -147,35 +166,50 @@
     table = restriction(nz, pad_z, weight_beside)
     lanes_beside = np.stack([over_lanes(at_first(table)), over_lanes(table)])
     grow = interpolation(nz, pad_z)
-    wide = np.zeros((2, LANES, rhs * nz), np.float32)
-    for s in range(2):
-        for r in range(rhs):
-            wide[s, r * pad_z:(r + 1) * pad_z, r * nz:(r + 1) * nz] = grow[s].T
-    wide = wide.reshape(2 * LANES, rhs * nz)
+    pack = rhs // 2
+    wide = np.zeros((rhs * nz, rhs * pad_z + TILE), np.float32)
+    for r in range(rhs):
+        wide[r * nz:(r + 1) * nz, r * pad_z:(r + 1) * pad_z] = grow[0]
+        wide[r * nz:(r + 1) * nz, rhs * pad_z + r % 2 * pack + r // 2] = grow[1][:, 0]
     tall_of = interpolation(ny, pad_y)
     slab_rows = side * pad_y
     face_rows = up_to(side, TILE)
     tall = np.zeros(((side + 1) * ny, slab_rows + pad_y + 2 * face_rows), np.float32)
+    cuts = face_cuts(side, ny // 4, nz // 4)
+    beyond = np.zeros((TILE, up_to(cuts["end"], LANES)), np.float32)
+    beyond[:2] = -1.0
+    sizes = (side, ny // 4, nz // 4)
+    for step in RIMS:
+        ranges = [range(1) if d else range(n) for d, n in zip(step, sizes)]
+        for at, (x, y, z) in enumerate(itertools.product(*ranges)):
+            if step[1]:
+                row = slab_rows + pad_y + (face_rows if step[0] else x)
+            else:
+                row = slab_rows + y if step[0] else x * pad_y + y
+            slot = cuts[step][2] + at
+            beyond[0, slot] = row
+            beyond[1, slot] = -1 if step[2] else z
+            beyond[2, slot] = step[2]
     for at in range(side + 1):
         here = slice(at * ny, (at + 1) * ny)
         tall[here, at * pad_y:(at + 1) * pad_y] = tall_of[0]
-        beyond = slab_rows + pad_y + (at if at < side else face_rows)
-        tall[here, beyond] = tall_of[1][:, 0]
-    return rows, lanes, lanes_beside, wide, tall
+        corner = slab_rows + pad_y + (at if at < side else face_rows)
+        tall[here, corner] = tall_of[1][:, 0]
+    return rows, lanes, lanes_beside, wide, tall, beyond
 
 
 def kernel(
     sizes,
     right_ref, u_ref, coef_ref, order_ref, leaf_ref, first_ref, second_ref, top_ref,
     fs_ref, ft_ref, st_ref, rows_first, rows_second, rows_top,
-    mat_rows, mat_lanes, mat_beside, mat_wide, mat_tall, blank,
+    mat_rows, mat_lanes, mat_beside, mat_wide, mat_tall, mat_beyond, blank,
     out_ref,
     right_in, u_in, coef_in, order_in, leaf_in, first_in, second_in, top_in,
-    fs_in, ft_in, st_in, rows_in, m_rows, m_lanes, m_beside, m_wide, m_tall,
-    leaf_split, link_split, fs_seat, ftst_seat, row_seat, rows0, rows1, big, w0, w1, zed, kay,
+    fs_in, ft_in, st_in, rows_in, m_rows, m_lanes, m_beside, m_wide, m_tall, m_beyond,
+    leaf_split, link_split, fs_seat, ftst_seat, row_seat, rows0, rows1, big, w0, w1, zed, kay, face_hot, back_hot, face_out, face_in, base_out, base_in, face_top, upper,
     packed, shares, share_in, prev, scatter_out, scatter_in, gather_in, top_all, val,
-    picked, slots, order_seat, ordered, rim, face, stage, k_own, k_all,
-    in_sem, ready, share_recv, rim_recv, prev_recv, k_sem, s_recv, g_recv,
+    picked, slots, order_seat, ordered, stage, k_own, k_all,
+    in_sem, ready, share_recv, face_recv, base_recv, upper_recv, prev_recv, k_sem, s_recv, g_recv,
 ):
     rhs, nx, ny, nz = u_in.shape
     side = nx // 4
@@ -293,6 +327,7 @@
     load("st", st_ref, st_in)
     load("m_wide", mat_wide, m_wide)
     load("m_tall", mat_tall, m_tall)
+    load("m_beyond", mat_beyond, m_beyond)
 
     share_at = [0]
     for step in SHARES:
@@ -303,22 +338,20 @@
         def _():
             part = pl.ds(share_at[n], share_at[n + 1] - share_at[n])
             pltpu.make_async_copy(
-                blank.at[pl.ds(0, share_at[n + 1] - share_at[n])], share_in.at[part], share_recv
+                blank.at[pl.ds(0, share_at[n + 1] - share_at[n]), pl.ds(0, LANES)], share_in.at[part], share_recv
             ).start()
-    face_rows = face.shape[0]
-
-    def rim_place(step):
-        dx, dy, dz = step
-        if dy:
-            return face_rows, main + pad_y + (face_rows if dx else 0)
-        return (pad_y, main) if dx else (main, 0)
-
+    cuts = face_cuts(side, side_y, side_z)
+    back_width = widths[1] + widths[0]
     for n, step in enumerate(RIMS):
         @pl.when(jnp.logical_not(valid(step, 1)))
         def _():
-            rows, at = rim_place(step)
+            _, rows, at = cuts[step]
             pltpu.make_async_copy(
-                blank.at[pl.ds(0, rows)], rim.at[step[2], pl.ds(at, rows)], rim_recv
+                blank.at[pl.ds(0, rows), pl.ds(0, back_width)],
+                face_in.at[pl.ds(at, rows), pl.ds(0, back_width)], face_recv
+            ).start()
+            pltpu.make_async_copy(
+                blank.at[pl.ds(0, TILE), pl.ds(0, base_out.shape[1])], base_in.at[n], base_recv
             ).start()
 
     def clear(ref):
@@ -362,6 +395,11 @@
         @pl.when(me[shift_axis[level]] == 0)
         def _():
             clear(prev[level])
+
+    @pl.when(me["gx"] == n_gx - 1)
+    def _():
+        clear(upper)
+
     clear(k_own)
     for level in range(2):
         clear(scatter_out[level])
@@ -411,6 +449,24 @@
             loads[name].wait()
     pl.semaphore_wait(barrier, near_count)
 
+    prev_copies = []
+    for level in range(3):
+        axis = shift_axis[level]
+        target = dict(me)
+        target[axis] = (me[axis] + 1) % peers[axis]
+        copy = pltpu.make_async_remote_copy(
+            src_ref=rows_in[level], dst_ref=prev[level],
+            send_sem=in_sem.at[len(SHARES) + level], recv_sem=prev_recv.at[level],
+            device_id=target, device_id_type=MESH,
+        )
+        prev_copies.append(copy)
+
+    def send_prev(level):
+        @pl.when(me[shift_axis[level]] < peers[shift_axis[level]] - 1)
+        def _():
+            prev_copies[level].start()
+
+    send_prev(1)
     share_copies = []
     for n, step in enumerate(SHARES):
         dx, dy, dz = step
@@ -430,22 +486,8 @@
         def _():
             copy.start()
 
-    prev_copies = []
-    for level in range(3):
-        axis = shift_axis[level]
-        target = dict(me)
-        target[axis] = (me[axis] + 1) % peers[axis]
-        copy = pltpu.make_async_remote_copy(
-            src_ref=rows_in[level], dst_ref=prev[level],
-            send_sem=in_sem.at[len(SHARES) + level], recv_sem=prev_recv.at[level],
-            device_id=target, device_id_type=MESH,
-        )
-        prev_copies.append(copy)
-
-        @pl.when(me[axis] < peers[axis] - 1)
-        def _():
-            copy.start()
-
+    send_prev(0)
+    send_prev(2)
     relay(0)
 
     def keep(where, value, rows=None):
@@ -455,6 +497,9 @@
         else:
             where[0][rows, :] = high
             where[1][rows, :] = low
+
+    def keep_sum(pair):
+        return pair[0][...].astype(f32) + pair[1][...].astype(f32)
 
     def rows_of(raw):
         return raw[:, 0, :] if len(raw.shape) == 3 else raw[...]
@@ -508,8 +553,31 @@
         (near & (second == 0)).astype(f32),
         (near & (second == side_y - 1)).astype(f32),
     ], 0)
-    face_hot = ((row_iota(face_rows) == first) & (second == 0)).astype(f32)
-    back_hot = jnp.concatenate([main_hot, face_hot], 0)
+    pieces = []
+    for n, value, zero in (
+        (0, second * side_z + third, first), (1, first * side_z + third, second),
+        (2, first * side_y + second, third), (3, second, first + third * side), (4, first, second + third * side),
+    ):
+        span = cuts["starts"][n + 1] - cuts["starts"][n]
+        pieces.append(((row_iota(span) == value) & (zero == 0)).astype(f32))
+    face_hot[...] = jnp.concatenate(pieces, 0).astype(bf16)
+    clear(back_hot)
+    back_hot[:main, :cells] = main_hot.astype(bf16)
+    back_rows = m_tall.shape[1]
+    beyond_width = m_beyond.shape[1]
+    beyond_id = lax.broadcasted_iota(jnp.int32, (back_rows, beyond_width), 0).astype(f32)
+    back_hot[:back_rows, cells:] = (beyond_id == m_beyond[0:1, :]).astype(f32).astype(bf16)
+    z_id = lax.broadcasted_iota(jnp.int32, (pad_z, cells), 0).astype(f32)
+    beyond_z = lax.broadcasted_iota(jnp.int32, (pad_z, beyond_width), 0).astype(f32)
+    z_hot = jnp.concatenate([
+        (z_id == third).astype(f32), (beyond_z == m_beyond[1:2, :]).astype(f32)
+    ], 1)
+    z_beyond = jnp.concatenate([jnp.zeros((1, cells), f32), m_beyond[2:3, :]], 1)
+    clear(zed[0])
+    clear(zed[1])
+    clear(val)
+    clear(ordered)
+    clear(base_out)
     lane_id = lax.broadcasted_iota(jnp.int32, (LANES, cells), 0).astype(f32)
 
     def lane_hot(r):
@@ -527,7 +595,6 @@
             row_seat[level][:, d * PITCH:d * PITCH + span] = value[:, d * span:(d + 1) * span]
         return row_seat[level][...]
 
-    relay(1)
     links = dot_back(rows_of(leaf_in), link_split)
     wait_prev(0)
     own0 = seat_lanes(rows_of(rows_in[0]), 0)
@@ -558,7 +625,7 @@
             buffer.at[pl.ds(0, count - 1)], buffer.at[pl.ds(0, count - 1)], sem
         )
 
-    relay(2)
+    relay(1)
     wait_prev(1)
     keep(rows1, seat_lanes(rows_of(prev[1]), 1), slice(seats[1], seats[1] + spans[1]))
     k_own[...] = dot(fs_seat[...], rows1)
@@ -623,6 +690,19 @@
         into, own = gather_in[level], stage[level]
         mine = place(group)
         own[...] = value
+        if level == 1:
+            for target in itertools.product(range(peers["gy"]), range(n_gz)):
+                @pl.when(me["gx"] > 0)
+                def _():
+                    pltpu.make_async_remote_copy(
+                        src_ref=own, dst_ref=upper.at[mine],
+                        send_sem=in_sem.at[len(SHARES) + 9], recv_sem=upper_recv,
+                        device_id={
+                            "gx": me["gx"] - 1, "gy": turned["gy"][-target[0]],
+                            "gz": turned["gz"][-target[1]],
+                        },
+                        device_id_type=MESH,
+                    ).start()
 
         def send(target, d):
             pltpu.make_async_remote_copy(
@@ -645,6 +725,50 @@
     keep(kay, k_all[...].reshape(n_gz * PITCH, k_own.shape[1]))
     scatter(1, base1 - dot(terms0, kay), PITCH, 0)
     scatter(0, terms0, PITCH, PITCH)
+    relay(2)
+    w0_value = keep_sum(w0)
+    gap_width, lead_width = widths[1], widths[0]
+    gap_part = halves(keep_sum(w1) - dot(w0_value, kay))
+    lead_part = (w0[0][...], w0[1][...])
+    lead_at = 2 * gap_width
+
+    def lead_cut(dx, dy):
+        at = lead_at + (2 * dx + dy) * lead_width
+        return slice(at, at + lead_width)
+
+    def gap_cut(dx):
+        return slice(dx * gap_width, (dx + 1) * gap_width)
+
+    for part in range(2):
+        zed[part][:at_top, gap_cut(0)] = gap_part[part]
+        zed[part][:at_top, lead_cut(0, 0)] = lead_part[part]
+    hot = face_hot[:, :at_top]
+    face_out[:, :gap_width] = single(hot, gap_part[0]) + single(hot, gap_part[1])
+    face_out[:, gap_width:back_width] = single(hot, lead_part[0]) + single(hot, lead_part[1])
+    for n, step in enumerate(SHARES):
+        @pl.when(valid(step, 1))
+        def _():
+            share_copies[n].wait_send()
+    face_copies = []
+    base_copies = []
+    for n, step in enumerate(RIMS):
+        start, rows, at = cuts[step]
+        face_copies.append(pltpu.make_async_remote_copy(
+            src_ref=face_out.at[pl.ds(start, rows), pl.ds(0, back_width)],
+            dst_ref=face_in.at[pl.ds(at, rows), pl.ds(0, back_width)],
+            send_sem=in_sem.at[n], recv_sem=face_recv,
+            device_id=toward(step, -1), device_id_type=MESH,
+        ))
+        base_copies.append(pltpu.make_async_remote_copy(
+            src_ref=base_out, dst_ref=base_in.at[n],
+            send_sem=in_sem.at[len(RIMS) + n], recv_sem=base_recv,
+            device_id=toward(step, -1), device_id_type=MESH,
+        ))
+
+        @pl.when(valid(step, -1))
+        def _():
+            face_copies[n].start()
+
     leaf_rhs = picked[:, :leaf]
     lows = dot(leaf_rhs, halves(links[:, 2 * (seats[0] + seats[1]):]))
     pair2 = 2 * seats[2]
@@ -667,11 +791,16 @@
         relay(step)
     scatter(2, base2 - dot(second_own[:, :2 * PITCH], queue_rows), spans[2], 0)
     both_own = (first_own + second_own)[:, :2 * PITCH]
-    w0_value = w0[0][...].astype(f32) + w0[1][...].astype(f32)
-    gap_width = widths[1]
-    high, low = halves(w1_value - dot(w0_value, kay))
-    zed[0][:, :gap_width], zed[1][:, :gap_width] = high, low
-    zed[0][:, gap_width:], zed[1][:, gap_width:] = w0[0][...], w0[1][...]
+    top_links = links[:, 2 * (seats[0] + seats[1]):]
+    link_high, link_low = halves(top_links)
+    hot = face_hot[:, :leaf]
+    keep(face_top, -(single(hot, link_high) + single(hot, link_low)))
+    for part in range(1):
+        face_top[part][:, :spans[2]] = (
+            face_top[part][:, :spans[2]].astype(f32) + face_hot[:, at_top:at_top + spans[2]].astype(f32)
+        ).astype(bf16)
+    leaf_base = dot_back(leaf_solved, leaf_split)
+    base0 = dot_exact(leaf_base, hot, single_back)
     top_own = scatter_end(2)
     gather(2, top_own)
     into = gather_end(2)
@@ -680,11 +809,27 @@
         top_all[:pack, at] = into[d, :, :spans[2]]
         top_all[pack:, at] = into[d, :, LANES // 2:LANES // 2 + spans[2]]
     solved = dot_back(top_all[...], big)
-    gather(1, jnp.concatenate([
-        both_own - solved[:, LANES:LANES + 2 * PITCH], jnp.zeros((rhs, LANES - 2 * PITCH), f32)
-    ], 1))
-    top_link = (link_split[0].at[pl.ds(link_at[2], pair2)], link_split[1].at[pl.ds(link_at[2], pair2)])
-    base = dot_back(leaf_solved - dot(solved[:, :pair2], top_link), leaf_split)
+    gap = both_own - solved[:, LANES:LANES + 2 * PITCH]
+    gather(1, jnp.concatenate([gap[:pack], gap[pack:]], 1))
+    top_pair = solved[:, :pair2]
+    base_out[:rhs, :face_hot.shape[0]] = base0 + dot_back(top_pair, face_top)
+    for n, step in enumerate(RIMS):
+        @pl.when(valid(step, -1))
+        def _():
+            base_copies[n].start()
+
+    base = leaf_base - dot_back(top_pair, halves(top_links))
+    arrived = face_in.at[pl.ds(0, sum(cuts[step][1] for step in RIMS))]
+    pltpu.make_async_copy(arrived, arrived, face_recv).wait()
+    for n, step in enumerate(RIMS):
+        dx, dy, dz = step
+        _, rows, at = cuts[step]
+        where = slice(cells + at, cells + at + rows)
+        value = face_in[at:at + rows]
+        for part, piece in zip(zed, halves(value[:, :gap_width])):
+            part[where, gap_cut(dx)] = piece
+        for part, piece in zip(zed, halves(value[:, gap_width:])):
+            part[where, lead_cut(dx, dy)] = piece
 
     for level in range(3):
         @pl.when(me[shift_axis[level]] < peers[shift_axis[level]] - 1)
@@ -694,59 +839,59 @@
         all_slots(scatter_out[level], s_send(level), counts[level]).wait()
     all_slots(k_all, in_sem.at[len(SHARES) + 3], n_gz).wait()
     all_slots(gather_in[2], g_send(2), counts[2]).wait()
-    for n, step in enumerate(SHARES):
-        @pl.when(valid(step, 1))
-        def _():
-            share_copies[n].wait_send()
-
-    into = gather_end(1)
-    clear(val)
-    for d in range(counts[1]):
-        val[:, d * PITCH:d * PITCH + spans[1]] = into[d, :, :spans[1]]
-    for d in range(n_gz):
-        at = gap_width + d * PITCH
-        val[:, at:at + spans[0]] = into[me["gy"] * n_gz + d, :, PITCH:PITCH + spans[0]]
-    back = dot_back(val[...], zed)
-    clear(ordered)
-    ordered[:, :at_top] = back
-    ordered[:, :leaf] = back[:, :leaf] + base
-    ordered[:, at_top:at_top + spans[2]] = solved[:, :spans[2]]
-
-    cells_back = None
-    for r in range(rhs):
-        term = dot_exact(back_hot * ordered[slot(r):slot(r) + 1, :], lane_hot(r), single_back)
-        cells_back = term if cells_back is None else cells_back + term
-    rim[0, 0:main] = cells_back[:main]
-    face[...] = cells_back[main:]
-
-    rim_copies = []
-    for n, step in enumerate(RIMS):
-        dx, dy, dz = step
-        rows, at = rim_place(step)
-        copy = pltpu.make_async_remote_copy(
-            src_ref=face if dy else rim.at[0, pl.ds(0, rows)],
-            dst_ref=rim.at[dz, pl.ds(at, rows)],
-            send_sem=in_sem.at[n], recv_sem=rim_recv,
-            device_id=toward(step, -1), device_id_type=MESH,
-        )
-        rim_copies.append(copy)
-
-        @pl.when(valid(step, -1))
-        def _():
-            copy.start()
-
-    all_slots(gather_in[1], g_send(1), counts[1]).wait()
-    arrived = share_in.at[pl.ds(0, 2 * rim.shape[1] - main)]
-    pltpu.make_async_copy(arrived, arrived, rim_recv).wait()
-
-    wide = dot_exact(jnp.concatenate([rim[0], rim[1]], 1), m_wide[...])
-    high, low = halves(wide)
-    out_ref[...] = single(m_tall[...], high) + single(m_tall[...], low)
-
     for n, step in enumerate(RIMS):
         @pl.when(valid(step, -1))
         def _():
-            rim_copies[n].wait_send()
+            face_copies[n].wait_send()
+
+    into = gather_end(1)
+    @pl.when(me["gx"] < n_gx - 1)
+    def _():
+        pltpu.make_async_copy(upper, upper, upper_recv).wait()
+
+    far_gy = jnp.minimum(me["gy"] + 1, peers["gy"] - 1)
+    middle = LANES // 2
+    for dx, source in enumerate((into, upper)):
+        for d in range(counts[1]):
+            at = dx * gap_width + d * PITCH
+            val[:pack, at:at + spans[1]] = source[d, :, :spans[1]]
+            val[pack:, at:at + spans[1]] = source[d, :, middle:middle + spans[1]]
+        for dy, gy in enumerate((me["gy"], far_gy)):
+            for d in range(n_gz):
+                at = lead_at + (2 * dx + dy) * lead_width + d * PITCH
+                lead = source[gy * n_gz + d]
+                val[:pack, at:at + spans[0]] = lead[:, PITCH:PITCH + spans[0]]
+                val[pack:, at:at + spans[0]] = lead[:, middle + PITCH:middle + PITCH + spans[0]]
+    back = dot_back(val[...], zed)
+    pltpu.make_async_copy(base_in, base_in, base_recv).wait()
+    ordered[:rhs, :at_top] = back[:, :at_top]
+    ordered[:rhs, :leaf] = back[:, :leaf] + base
+    ordered[:rhs, at_top:at_top + spans[2]] = solved[:, :spans[2]]
+    for n, step in enumerate(RIMS):
+        start, rows, at = cuts[step]
+        where = slice(cells + at, cells + at + rows)
+        ordered[:rhs, where] = back[:, where] + base_in[n, :rhs, start:start + rows]
+
+    value = ordered[...]
+    spread = jnp.concatenate(
+        [z_hot * value[slot(r):slot(r) + 1] for r in range(rhs)] + [z_beyond * value], 0
+    )
+    cells_back = dot_exact(spread, back_hot[:back_rows], single_back)
+    high, low = halves(cells_back)
+    wide = single(m_wide[...], high) + single(m_wide[...], low)
+    high, low = halves(wide)
+    out_ref[...] = single_back(m_tall[...], high) + single_back(m_tall[...], low)
+
+    all_slots(gather_in[1], g_send(1), counts[1]).wait()
+
+    @pl.when(me["gx"] > 0)
+    def _():
+        pltpu.make_async_copy(upper, upper, in_sem.at[len(SHARES) + 9]).wait()
+
+    for n, step in enumerate(RIMS):
+        @pl.when(valid(step, -1))
+        def _():
+            base_copies[n].wait_send()
 
 
 def spread_kernel(grown_ref, out_ref, held, sem):
@@ -779,6 +924,7 @@
     pad_y = up_to(ny // 4, TILE)
     pad_z = LANES // rhs // 4 if nz // 4 <= LANES // rhs // 4 else LANES // rhs
     mats = [jnp.asarray(m, bf16) for m in constants(rhs, ny, nz, side, pad_y, pad_z)]
+    mats[-1] = mats[-1].astype(f32)
     flip = lambda m: jnp.swapaxes(m, -1, -2)
     flat = lambda m: m.reshape(m.shape[-2:])
     single_rows = lambda m: m.reshape(m.shape[-2], 1, m.shape[-1])
@@ -810,8 +956,12 @@
     edge_rows = up_to(slabs, TILE)
     face_rows = up_to(side, TILE)
     main = side * pad_y
-    blank = np.zeros((main + TILE, LANES), np.float32)
-    blank[main:] = 1.0
+    cuts = face_cuts(side, ny // 4, nz // 4)
+    back_width = widths[0] + widths[1]
+    face_width = up_to(cuts["rows"], LANES)
+    blank_rows = max([main] + [cuts[step][1] for step in RIMS])
+    blank = np.zeros((blank_rows + TILE, max(back_width, face_width)), np.float32)
+    blank[blank_rows:] = 1.0
     operands = (right_side, iterate, coefficient, *matrices, *rows, *mats, jnp.asarray(blank))
 
     def share_shape(step):
@@ -822,6 +972,7 @@
     anywhere = pl.BlockSpec(memory_space=pl.ANY)
     links = 2 * sum(seats)
     packs = (rhs, rhs, rhs // 2)
+    gather_packs = (rhs, rhs // 2, rhs // 2)
     big_rows = LANES + 2 * PITCH
     grown = pl.pallas_call(
         functools.partial(kernel, sizes),
@@ -832,7 +983,7 @@
             like(right_side), like(iterate), like(coefficient), *[like(m) for m in matrices],
             [like(m) for m in rows],
             pltpu.VMEM(mats[0].shape[1:], bf16), like(mats[1]),
-            pltpu.VMEM(mats[2].shape[1:], bf16), like(mats[3]), like(mats[4]),
+            pltpu.VMEM(mats[2].shape[1:], bf16), like(mats[3]), like(mats[4]), like(mats[5]),
             split(leaf, leaf),
             split(links, leaf),
             vmem(PITCH, 2 * seats[1]),
@@ -843,29 +994,33 @@
             split(big_rows, widths[2]),
             split(at_top, widths[0]),
             split(at_top, widths[1]),
-            split(at_top, widths[1] + widths[0]),
+            split(slots + cuts["end"], 2 * widths[1] + 4 * widths[0]),
             split(counts[0] * PITCH, widths[1]),
+            pltpu.VMEM((cuts["rows"], slots), bf16),
+            pltpu.VMEM((up_to(main + pad_y + 2 * face_rows, 16), slots + mats[5].shape[1]), bf16),
+            vmem(cuts["rows"], back_width), vmem(cuts["end"], back_width),
+            vmem(TILE, face_width), vmem(len(RIMS), TILE, face_width),
+            split(cuts["rows"], 2 * seats[2]),
+            vmem(counts[1], rhs // 2, LANES),
             vmem(2 * slabs * ny, rhs * nz),
             vmem(3, slabs * pad_y + 2 * edge_rows, LANES),
             vmem(sum(share_shape(step)[0] for step in SHARES), LANES),
             [like(m) for m in rows],
             [vmem(n, p, LANES) for n, p in zip(counts, packs)],
             [vmem(n, p, LANES) for n, p in zip(counts, packs)],
-            [vmem(n, p, LANES) for n, p in zip(counts, packs)],
+            [vmem(n, p, LANES) for n, p in zip(counts, gather_packs)],
             vmem(rhs, widths[2]),
-            vmem(rhs, widths[1] + widths[0]),
+            vmem(rhs, 2 * widths[1] + 4 * widths[0]),
             vmem(rhs, slots),
             vmem(rhs, 2 * seats[2]),
             vmem(1, slots),
-            vmem(rhs, slots),
-            vmem(2, main + pad_y + 2 * face_rows, LANES),
-            vmem(face_rows, LANES),
-            [vmem(p, LANES) for p in packs],
+            vmem(TILE, slots + mats[5].shape[1]),
+            [vmem(p, LANES) for p in gather_packs],
             vmem(PITCH, widths[1]),
             vmem(counts[0], PITCH, widths[1]),
-            dma(max(len(SHARES) + 9, 2 * rhs + len(operands) - 3)),
+            dma(max(len(SHARES) + 10, 2 * rhs + len(operands) - 3)),
             pltpu.SemaphoreType.REGULAR((2, max(peers["gx"] - 1, 1))),
-            pltpu.SemaphoreType.DMA, pltpu.SemaphoreType.DMA, dma(3), dma(1), dma(3), dma(2),
+            *[pltpu.SemaphoreType.DMA] * 4, dma(3), dma(1), dma(3), dma(2),
         ],
         compiler_params=pltpu.CompilerParams(has_side_effects=True, collective_id=0),
     )(*operands)

time: 30.6 us -> 28.2 us (0.922)
  Pallas kernels: 30.4 us -> 28.1 us
    pallas_call x1, Pallas kernels: 29.3 us -> 27 us  [per_device(): pl.pallas_call(functools.partial(kernel, sizes), out_shape=pltpu.VMEM(((s...]
where the time goes in v4:
time: 28.2 us; the launch traced here: 28.1 us
  Pallas kernels  28.1 us (100%)
    pallas_call x1, Pallas kernels, per_device(): pl.pallas_call(functools.partial(kernel, sizes), out_shape=pltpu.VMEM(((s...  27 us
    pallas_call x1, Pallas kernels, per_device(): pl.pallas_call(spread_kernel, out_shape=jax.ShapeDtypeStruct(iterate.shap...  1.09 us

profile of v4, /device:TPU:0, one launch (start us, length us, event | category | flops | bytes accessed | tf_op | source)
XLA Modules:
  0.0 28.1 jit_solution(13008069109425907148)
XLA Ops:
  0.0 27.0 %shard_map.199.grown_ref = f32[168,96]{1,0:T(8,128)S(1)} custom-call(f32[4,24,24,24]{3,2,1,0:T(8,128)} %right_ref.1, f32[4,24,24,24]{3,2,1,0:T(8,128)} %u_ref.1, f32[24,24,24]{2,1,0:T(8,128)} %coef_ref.1, s32[1,216]{1,0:T(1,128)} %bitcast.29, f32[125,1,125]{2,1,0:T(1,128)} %bitcast.20, f32[50,1,125]{2,1,0:T(1,128)} %bitcast.24, f32[60,1,125]{2,1,0:T(1,128)} %bitcast.22, ...), custom_call_target="tpu_custom_call" | custom-call | tf_op jit(solution)/shard_map/pallas_call | solution.py:977
  27.0 1.1 %shard_map.200 = f32[4,24,24,24]{3,2,1,0:T(8,128)} custom-call(f32[168,96]{1,0:T(8,128)S(1)} %shard_map.199.grown_ref), custom_call_target="tpu_custom_call" | custom-call | tf_op jit(solution)/shard_map/pallas_call | solution.py:1027

commit v5 on v4

--- a/solution.py
+++ b/solution.py
@@ -28,7 +28,7 @@
 ]
 SHARES.sort(key=lambda step: -2 * abs(step[1]) - abs(step[0]))
 RIMS = [(i, j, k) for i in (0, 1) for j in (0, 1) for k in (0, 1) if (i, j, k) != (0, 0, 0)]
-RIMS.sort(key=lambda step: -2 * step[1] - step[0])
+RIMS.sort(key=lambda step: -2 * step[0] - step[1])
 
 
 def up_to(n, unit):
@@ -126,11 +126,15 @@
         (1, 0, 1): (3, 3), (0, 1, 1): (4, 4), (1, 1, 1): (0, None),
     }
     cuts, at = {"rows": starts[-1], "starts": starts}, 0
-    for step in RIMS:
-        face, size = source[step]
-        rows = up_to(side_z if size is None else faces[size], TILE)
-        cuts[step] = (starts[face], rows, at)
-        at += up_to(rows, 16)
+    for dx in (0, 1):
+        for step in RIMS:
+            if step[0] == dx:
+                face, size = source[step]
+                rows = up_to(side_z if size is None else faces[size], TILE)
+                cuts[step] = (starts[face], rows, at)
+                at += up_to(rows, 16)
+        at = up_to(at, LANES)
+        cuts[dx] = at
     cuts["end"] = at
     return cuts
 
@@ -166,11 +170,9 @@
     table = restriction(nz, pad_z, weight_beside)
     lanes_beside = np.stack([over_lanes(at_first(table)), over_lanes(table)])
     grow = interpolation(nz, pad_z)
-    pack = rhs // 2
-    wide = np.zeros((rhs * nz, rhs * pad_z + TILE), np.float32)
-    for r in range(rhs):
-        wide[r * nz:(r + 1) * nz, r * pad_z:(r + 1) * pad_z] = grow[0]
-        wide[r * nz:(r + 1) * nz, rhs * pad_z + r % 2 * pack + r // 2] = grow[1][:, 0]
+    wide = np.zeros((nz, 2 * TILE), np.float32)
+    wide[:, :pad_z] = grow[0]
+    wide[:, pad_z] = grow[1][:, 0]
     tall_of = interpolation(ny, pad_y)
     slab_rows = side * pad_y
     face_rows = up_to(side, TILE)
@@ -195,7 +197,7 @@
         tall[here, at * pad_y:(at + 1) * pad_y] = tall_of[0]
         corner = slab_rows + pad_y + (at if at < side else face_rows)
         tall[here, corner] = tall_of[1][:, 0]
-    return rows, lanes, lanes_beside, wide, tall, beyond
+    return rows / 16.0, lanes, lanes_beside, wide, tall, beyond
 
 
 def kernel(
@@ -206,8 +208,8 @@
     out_ref,
     right_in, u_in, coef_in, order_in, leaf_in, first_in, second_in, top_in,
     fs_in, ft_in, st_in, rows_in, m_rows, m_lanes, m_beside, m_wide, m_tall, m_beyond,
-    leaf_split, link_split, fs_seat, ftst_seat, row_seat, rows0, rows1, big, w0, w1, zed, kay, face_hot, back_hot, face_out, face_in, base_out, base_in, face_top, upper,
-    packed, shares, share_in, prev, scatter_out, scatter_in, gather_in, top_all, val,
+    leaf_split, link_split, fs_seat, ftst_seat, row_seat, rows0, rows1, big, w0, w1, zed, zed_up, kay, z_wide, face_hot, back_hot, face_out, face_in, base_out, base_in, face_top, upper,
+    packed, shares, share_in, prev, scatter_out, scatter_in, gather_in, top_all, val, val_up,
     picked, slots, order_seat, ordered, stage, k_own, k_all,
     in_sem, ready, share_recv, face_recv, base_recv, upper_recv, prev_recv, k_sem, s_recv, g_recv,
 ):
@@ -306,6 +308,12 @@
     for r in range(rhs):
         load(("u", r), u_ref.at[r], u_in.at[r])
         load(("right", r), right_ref.at[r], right_in.at[r])
+    for_others(groups[1], greet)
+    for step in itertools.product((1, -1), SIDES, SIDES):
+        @pl.when(valid(step, 1))
+        def _():
+            greet(toward(step, 1), 0)
+
     load("m_rows", mat_rows.at[at_y], m_rows)
     load("m_lanes", mat_lanes, m_lanes)
     load("m_beside", mat_beside.at[at_z], m_beside)
@@ -351,17 +359,11 @@
                 face_in.at[pl.ds(at, rows), pl.ds(0, back_width)], face_recv
             ).start()
             pltpu.make_async_copy(
-                blank.at[pl.ds(0, TILE), pl.ds(0, base_out.shape[1])], base_in.at[n], base_recv
+                blank.at[pl.ds(0, TILE), pl.ds(0, base_out.shape[1])], base_in.at[n], base_recv.at[step[0]]
             ).start()
 
     def clear(ref):
         ref[...] = jnp.zeros(ref.shape, ref.dtype)
-
-    for_others(groups[1], greet)
-    for step in itertools.product((1, -1), SIDES, SIDES):
-        @pl.when(valid(step, 1))
-        def _():
-            greet(toward(step, 1), 0)
 
     def beside(a):
         return jnp.where(me[a] > 0, 1, 0) + jnp.where(me[a] < peers[a] - 1, 1, 0)
@@ -406,34 +408,42 @@
 
     half = slabs * ny
     loads["coef"].wait()
+    coef_in[...] = coef_in[...] + 6.0
     for r in range(rhs):
         loads["u", r].wait()
         loads["right", r].wait()
-        acc_p = {}
-        acc_u = {}
-
-        def add(acc, at, factor, value):
-            term = factor * value
-            acc[at] = acc[at] + term if at in acc else term
-
-        for x in range(nx):
-            u = u_in[r, x]
-            q = right_in[r, x] - (6.0 + coef_in[x]) * u
-            for at in range(-1, side + 1):
-                k = x - 4 * at
-                if weight(k):
-                    add(acc_p, at, weight(k), q)
-                    add(acc_u, at, weight(k), u)
-                if at == 0 and x == 0:
-                    below = jnp.where(me["gx"] > 0, weight(-1), 0.0)
-                    add(acc_p, at, weight(1) + below, u)
-                elif weight_beside(k):
-                    add(acc_p, at, weight_beside(k), u)
-        for at in range(-1, side + 1):
-            rows = slice((at + 1) * ny, (at + 2) * ny)
-            packed[rows, r * nz:(r + 1) * nz] = acc_p[at]
-            rows = slice(half + (at + 1) * ny, half + (at + 2) * ny)
-            packed[rows, r * nz:(r + 1) * nz] = acc_u.get(at, jnp.zeros((ny, nz), f32))
+        def put(at, value, lower):
+            rows = slice((at + 1) * ny + lower, (at + 2) * ny + lower)
+            packed[rows, r * nz:(r + 1) * nz] = value
+
+        def source(x):
+            q = right_in[r, x] - coef_in[x] * u_in[r, x]
+            if x > 0:
+                q = q + u_in[r, x - 1]
+            return q + u_in[r, x + 1] if x < nx - 1 else q
+
+        first = u_in[r, 0]
+        put(-1, first, 0)
+        put(-1, jnp.zeros((ny, nz), f32), half)
+        q_last = jnp.where(me["gx"] > 0, first, 0.0)
+        h_last, u_last, g_last = q_last, None, None
+        for at in range(side):
+            x = 4 * at
+            q = [source(x + k) for k in range(4)]
+            h = (q_last + q[1]) + (q[0] + q[0])
+            h_next = (q[1] + q[3]) + (q[2] + q[2])
+            put(at, (h_last + h_next) + (h + h), 0)
+            q_last, h_last = q[3], h_next
+            u = [u_in[r, x + k] for k in range(4)]
+            g = u[1] + (u[0] + u[0])
+            g = g if at == 0 else g + u_last
+            g_next = (u[1] + u[3]) + (u[2] + u[2])
+            g_sum = g_next + (g + g)
+            put(at, g_sum if at == 0 else g_sum + g_last, half)
+            u_last, g_last = u[3], g_next
+        h = q_last + (u_last + u_last)
+        put(side, h_last + (h + h), 0)
+        put(side, g_last + (u_last + u_last), half)
     loads["m_rows"].wait()
     loads["m_lanes"].wait()
     loads["m_beside"].wait()
@@ -570,12 +580,17 @@
     z_id = lax.broadcasted_iota(jnp.int32, (pad_z, cells), 0).astype(f32)
     beyond_z = lax.broadcasted_iota(jnp.int32, (pad_z, beyond_width), 0).astype(f32)
     z_hot = jnp.concatenate([
-        (z_id == third).astype(f32), (beyond_z == m_beyond[1:2, :]).astype(f32)
-    ], 1)
-    z_beyond = jnp.concatenate([jnp.zeros((1, cells), f32), m_beyond[2:3, :]], 1)
-    clear(zed[0])
-    clear(zed[1])
-    clear(val)
+        jnp.concatenate([
+            (z_id == third).astype(f32), (beyond_z == m_beyond[1:2, :]).astype(f32)
+        ], 1),
+        jnp.concatenate([
+            jnp.zeros((2 * TILE - pad_z, cells), f32),
+            jnp.broadcast_to(m_beyond[2:3, :], (2 * TILE - pad_z, beyond_width)),
+        ], 1),
+    ], 0)
+    z_wide[...] = single(m_wide[...], z_hot.astype(bf16))
+    for part in (*zed, *zed_up, val, val_up):
+        clear(part)
     clear(ordered)
     clear(base_out)
     lane_id = lax.broadcasted_iota(jnp.int32, (LANES, cells), 0).astype(f32)
@@ -730,18 +745,12 @@
     gap_width, lead_width = widths[1], widths[0]
     gap_part = halves(keep_sum(w1) - dot(w0_value, kay))
     lead_part = (w0[0][...], w0[1][...])
-    lead_at = 2 * gap_width
-
-    def lead_cut(dx, dy):
-        at = lead_at + (2 * dx + dy) * lead_width
-        return slice(at, at + lead_width)
-
-    def gap_cut(dx):
-        return slice(dx * gap_width, (dx + 1) * gap_width)
+    def lead_cut(dy):
+        return slice(gap_width + dy * lead_width, gap_width + (dy + 1) * lead_width)
 
     for part in range(2):
-        zed[part][:at_top, gap_cut(0)] = gap_part[part]
-        zed[part][:at_top, lead_cut(0, 0)] = lead_part[part]
+        zed[part][:at_top, :gap_width] = gap_part[part]
+        zed[part][:at_top, lead_cut(0)] = lead_part[part]
     hot = face_hot[:, :at_top]
     face_out[:, :gap_width] = single(hot, gap_part[0]) + single(hot, gap_part[1])
     face_out[:, gap_width:back_width] = single(hot, lead_part[0]) + single(hot, lead_part[1])
@@ -761,7 +770,7 @@
         ))
         base_copies.append(pltpu.make_async_remote_copy(
             src_ref=base_out, dst_ref=base_in.at[n],
-            send_sem=in_sem.at[len(RIMS) + n], recv_sem=base_recv,
+            send_sem=in_sem.at[len(RIMS) + n], recv_sem=base_recv.at[step[0]],
             device_id=toward(step, -1), device_id_type=MESH,
         ))
 
@@ -808,10 +817,10 @@
         at = slice(d * spans[2], (d + 1) * spans[2])
         top_all[:pack, at] = into[d, :, :spans[2]]
         top_all[pack:, at] = into[d, :, LANES // 2:LANES // 2 + spans[2]]
-    solved = dot_back(top_all[...], big)
-    gap = both_own - solved[:, LANES:LANES + 2 * PITCH]
+    top_value = top_all[...]
+    gap = both_own - dot_back(top_value, queue_rows)
     gather(1, jnp.concatenate([gap[:pack], gap[pack:]], 1))
-    top_pair = solved[:, :pair2]
+    top_pair = dot_back(top_value, rows2)
     base_out[:rhs, :face_hot.shape[0]] = base0 + dot_back(top_pair, face_top)
     for n, step in enumerate(RIMS):
         @pl.when(valid(step, -1))
@@ -824,12 +833,14 @@
     for n, step in enumerate(RIMS):
         dx, dy, dz = step
         _, rows, at = cuts[step]
-        where = slice(cells + at, cells + at + rows)
+        into = zed_up if dx else zed
+        begin = at - cuts[0] if dx else cells + at
+        where = slice(begin, begin + rows)
         value = face_in[at:at + rows]
-        for part, piece in zip(zed, halves(value[:, :gap_width])):
-            part[where, gap_cut(dx)] = piece
-        for part, piece in zip(zed, halves(value[:, gap_width:])):
-            part[where, lead_cut(dx, dy)] = piece
+        for part, piece in zip(into, halves(value[:, :gap_width])):
+            part[where, :gap_width] = piece
+        for part, piece in zip(into, halves(value[:, gap_width:])):
+            part[where, lead_cut(dy)] = piece
 
     for level in range(3):
         @pl.when(me[shift_axis[level]] < peers[shift_axis[level]] - 1)
@@ -845,40 +856,59 @@
             face_copies[n].wait_send()
 
     into = gather_end(1)
+    far_gy = jnp.minimum(me["gy"] + 1, peers["gy"] - 1)
+    middle = LANES // 2
+
+    def seat_values(into, source):
+        for d in range(counts[1]):
+            at = slice(d * PITCH, d * PITCH + spans[1])
+            into[:pack, at] = source[d, :, :spans[1]]
+            into[pack:, at] = source[d, :, middle:middle + spans[1]]
+        for dy, gy in enumerate((me["gy"], far_gy)):
+            for d in range(n_gz):
+                at = lead_cut(dy).start + d * PITCH
+                lead = source[gy * n_gz + d]
+                into[:pack, at:at + spans[0]] = lead[:, PITCH:PITCH + spans[0]]
+                into[pack:, at:at + spans[0]] = lead[:, middle + PITCH:middle + PITCH + spans[0]]
+
+    def wait_base(dx):
+        some = base_in.at[pl.ds(0, sum(step[0] == dx for step in RIMS))]
+        pltpu.make_async_copy(some, some, base_recv.at[dx]).wait()
+
+    def beyond_values(back, dx, begin):
+        for n, step in enumerate(RIMS):
+            if step[0] == dx:
+                start, rows, at = cuts[step]
+                where = slice(cells + at, cells + at + rows)
+                ordered[:rhs, where] = (
+                    back[:, at - begin:at - begin + rows] + base_in[n, :rhs, start:start + rows]
+                )
+
+    def over_cells(begin, end):
+        value = ordered[:, begin:end]
+        weights = z_wide[:, begin:end]
+        grown = jnp.concatenate([weights * value[slot(r):slot(r) + 1] for r in range(rhs)], 0)
+        return dot_exact(grown, back_hot[:back_rows, begin:end], single_back)
+
+    split_at = cells + cuts[0]
+    seat_values(val, into)
+    back = dot_back(val[...], zed)
+    ordered[:rhs, :at_top] = back[:, :at_top]
+    ordered[:rhs, :leaf] = back[:, :leaf] + base
+    ordered[:rhs, at_top:at_top + spans[2]] = top_pair[:, :spans[2]]
+    wait_base(0)
+    beyond_values(back[:, cells:], 0, 0)
+    wide = over_cells(0, split_at)
+
     @pl.when(me["gx"] < n_gx - 1)
     def _():
         pltpu.make_async_copy(upper, upper, upper_recv).wait()
 
-    far_gy = jnp.minimum(me["gy"] + 1, peers["gy"] - 1)
-    middle = LANES // 2
-    for dx, source in enumerate((into, upper)):
-        for d in range(counts[1]):
-            at = dx * gap_width + d * PITCH
-            val[:pack, at:at + spans[1]] = source[d, :, :spans[1]]
-            val[pack:, at:at + spans[1]] = source[d, :, middle:middle + spans[1]]
-        for dy, gy in enumerate((me["gy"], far_gy)):
-            for d in range(n_gz):
-                at = lead_at + (2 * dx + dy) * lead_width + d * PITCH
-                lead = source[gy * n_gz + d]
-                val[:pack, at:at + spans[0]] = lead[:, PITCH:PITCH + spans[0]]
-                val[pack:, at:at + spans[0]] = lead[:, middle + PITCH:middle + PITCH + spans[0]]
-    back = dot_back(val[...], zed)
-    pltpu.make_async_copy(base_in, base_in, base_recv).wait()
-    ordered[:rhs, :at_top] = back[:, :at_top]
-    ordered[:rhs, :leaf] = back[:, :leaf] + base
-    ordered[:rhs, at_top:at_top + spans[2]] = solved[:, :spans[2]]
-    for n, step in enumerate(RIMS):
-        start, rows, at = cuts[step]
-        where = slice(cells + at, cells + at + rows)
-        ordered[:rhs, where] = back[:, where] + base_in[n, :rhs, start:start + rows]
-
-    value = ordered[...]
-    spread = jnp.concatenate(
-        [z_hot * value[slot(r):slot(r) + 1] for r in range(rhs)] + [z_beyond * value], 0
-    )
-    cells_back = dot_exact(spread, back_hot[:back_rows], single_back)
-    high, low = halves(cells_back)
-    wide = single(m_wide[...], high) + single(m_wide[...], low)
+    seat_values(val_up, upper)
+    back = dot_back(val_up[...], zed_up)
+    wait_base(1)
+    beyond_values(back, 1, cuts[0])
+    wide = wide + over_cells(split_at, cells + cuts["end"])
     high, low = halves(wide)
     out_ref[...] = single_back(m_tall[...], high) + single_back(m_tall[...], low)
 
@@ -994,8 +1024,10 @@
             split(big_rows, widths[2]),
             split(at_top, widths[0]),
             split(at_top, widths[1]),
-            split(slots + cuts["end"], 2 * widths[1] + 4 * widths[0]),
+            split(slots + cuts[0], widths[1] + 2 * widths[0]),
+            split(cuts["end"] - cuts[0], widths[1] + 2 * widths[0]),
             split(counts[0] * PITCH, widths[1]),
+            vmem(nz, slots + mats[5].shape[1]),
             pltpu.VMEM((cuts["rows"], slots), bf16),
             pltpu.VMEM((up_to(main + pad_y + 2 * face_rows, 16), slots + mats[5].shape[1]), bf16),
             vmem(cuts["rows"], back_width), vmem(cuts["end"], back_width),
@@ -1010,7 +1042,8 @@
             [vmem(n, p, LANES) for n, p in zip(counts, packs)],
             [vmem(n, p, LANES) for n, p in zip(counts, gather_packs)],
             vmem(rhs, widths[2]),
-            vmem(rhs, 2 * widths[1] + 4 * widths[0]),
+            vmem(rhs, widths[1] + 2 * widths[0]),
+            vmem(rhs, widths[1] + 2 * widths[0]),
             vmem(rhs, slots),
             vmem(rhs, 2 * seats[2]),
             vmem(1, slots),
@@ -1020,7 +1053,7 @@
             vmem(counts[0], PITCH, widths[1]),
             dma(max(len(SHARES) + 10, 2 * rhs + len(operands) - 3)),
             pltpu.SemaphoreType.REGULAR((2, max(peers["gx"] - 1, 1))),
-            *[pltpu.SemaphoreType.DMA] * 4, dma(3), dma(1), dma(3), dma(2),
+            *[pltpu.SemaphoreType.DMA] * 2, dma(2), pltpu.SemaphoreType.DMA, dma(3), dma(1), dma(3), dma(2),
         ],
         compiler_params=pltpu.CompilerParams(has_side_effects=True, collective_id=0),
     )(*operands)

time: 28.2 us -> 27.8 us (0.986)
  Pallas kernels: 28.1 us -> 27.7 us
    pallas_call x1, Pallas kernels: 27 us -> 26.6 us  [per_device(): pl.pallas_call(functools.partial(kernel, sizes), out_shape=pltpu.VMEM(((s...]
where the time goes in v5:
time: 27.8 us; the launch traced here: 27.7 us
  Pallas kernels  27.7 us (100%)
    pallas_call x1, Pallas kernels, per_device(): pl.pallas_call(functools.partial(kernel, sizes), out_shape=pltpu.VMEM(((s...  26.6 us
    pallas_call x1, Pallas kernels, per_device(): pl.pallas_call(spread_kernel, out_shape=jax.ShapeDtypeStruct(iterate.shap...  1.09 us

profile of v5, /device:TPU:0, one launch (start us, length us, event | category | flops | bytes accessed | tf_op | source)
XLA Modules:
  0.0 27.7 jit_solution(15502766528213043336)
XLA Ops:
  0.0 26.6 %shard_map.199.grown_ref = f32[168,96]{1,0:T(8,128)S(1)} custom-call(f32[4,24,24,24]{3,2,1,0:T(8,128)} %right_ref.1, f32[4,24,24,24]{3,2,1,0:T(8,128)} %u_ref.1, f32[24,24,24]{2,1,0:T(8,128)} %coef_ref.1, s32[1,216]{1,0:T(1,128)} %bitcast.29, f32[125,1,125]{2,1,0:T(1,128)} %bitcast.20, f32[50,1,125]{2,1,0:T(1,128)} %bitcast.24, f32[60,1,125]{2,1,0:T(1,128)} %bitcast.22, ...), custom_call_target="tpu_custom_call" | custom-call | tf_op jit(solution)/shard_map/pallas_call | solution.py:1007
  26.6 1.1 %shard_map.200 = f32[4,24,24,24]{3,2,1,0:T(8,128)} custom-call(f32[168,96]{1,0:T(8,128)S(1)} %shard_map.199.grown_ref), custom_call_target="tpu_custom_call" | custom-call | tf_op jit(solution)/shard_map/pallas_call | solution.py:1060

commit v6 on v5

--- a/solution.py
+++ b/solution.py
@@ -206,14 +206,14 @@
     fs_ref, ft_ref, st_ref, rows_first, rows_second, rows_top,
     mat_rows, mat_lanes, mat_beside, mat_wide, mat_tall, mat_beyond, blank,
     out_ref,
-    right_in, u_in, coef_in, order_in, leaf_in, first_in, second_in, top_in,
+    fields_in, coef_in, order_in, leaf_in, first_in, second_in, top_in,
     fs_in, ft_in, st_in, rows_in, m_rows, m_lanes, m_beside, m_wide, m_tall, m_beyond,
     leaf_split, link_split, fs_seat, ftst_seat, row_seat, rows0, rows1, big, w0, w1, zed, zed_up, kay, z_wide, face_hot, back_hot, face_out, face_in, base_out, base_in, face_top, upper,
     packed, shares, share_in, prev, scatter_out, scatter_in, gather_in, top_all, val, val_up,
     picked, slots, order_seat, ordered, stage, k_own, k_all,
     in_sem, ready, share_recv, face_recv, base_recv, upper_recv, prev_recv, k_sem, s_recv, g_recv,
 ):
-    rhs, nx, ny, nz = u_in.shape
+    rhs, nx, ny, nz = u_ref.shape
     side = nx // 4
     side_y, side_z = ny // 4, nz // 4
     slabs = side + 2
@@ -306,8 +306,13 @@
 
     load("coef", coef_ref, coef_in)
     for r in range(rhs):
-        load(("u", r), u_ref.at[r], u_in.at[r])
-        load(("right", r), right_ref.at[r], right_in.at[r])
+        for n, whole_field in enumerate((u_ref, right_ref)):
+            pltpu.make_async_copy(
+                whole_field.at[r], fields_in.at[r, n], in_sem.at[len(loads)]
+            ).start()
+        loads["fields", r] = pltpu.make_async_copy(
+            fields_in.at[r], fields_in.at[r], in_sem.at[len(loads)]
+        )
     for_others(groups[1], greet)
     for step in itertools.product((1, -1), SIDES, SIDES):
         @pl.when(valid(step, 1))
@@ -410,19 +415,18 @@
     loads["coef"].wait()
     coef_in[...] = coef_in[...] + 6.0
     for r in range(rhs):
-        loads["u", r].wait()
-        loads["right", r].wait()
+        loads["fields", r].wait()
         def put(at, value, lower):
             rows = slice((at + 1) * ny + lower, (at + 2) * ny + lower)
             packed[rows, r * nz:(r + 1) * nz] = value
 
         def source(x):
-            q = right_in[r, x] - coef_in[x] * u_in[r, x]
+            q = fields_in[r, 1, x] - coef_in[x] * fields_in[r, 0, x]
             if x > 0:
-                q = q + u_in[r, x - 1]
-            return q + u_in[r, x + 1] if x < nx - 1 else q
-
-        first = u_in[r, 0]
+                q = q + fields_in[r, 0, x - 1]
+            return q + fields_in[r, 0, x + 1] if x < nx - 1 else q
+
+        first = fields_in[r, 0, 0]
         put(-1, first, 0)
         put(-1, jnp.zeros((ny, nz), f32), half)
         q_last = jnp.where(me["gx"] > 0, first, 0.0)
@@ -434,7 +438,7 @@
             h_next = (q[1] + q[3]) + (q[2] + q[2])
             put(at, (h_last + h_next) + (h + h), 0)
             q_last, h_last = q[3], h_next
-            u = [u_in[r, x + k] for k in range(4)]
+            u = [fields_in[r, 0, x + k] for k in range(4)]
             g = u[1] + (u[0] + u[0])
             g = g if at == 0 else g + u_last
             g_next = (u[1] + u[3]) + (u[2] + u[2])
@@ -455,7 +459,7 @@
         shares[t] = c[:, t * LANES:(t + 1) * LANES]
 
     for name in loads:
-        if name not in ("coef", "m_rows", "m_lanes", "m_beside") and name[0] not in ("u", "right"):
+        if name not in ("coef", "m_rows", "m_lanes", "m_beside") and name[0] != "fields":
             loads[name].wait()
     pl.semaphore_wait(barrier, near_count)
 
@@ -633,7 +637,7 @@
         return in_sem.at[len(SHARES) + 4 + level]
 
     def g_send(level):
-        return in_sem.at[len(SHARES) + 6 + level]
+        return in_sem.at[2 * len(RIMS) + level]
 
     def all_slots(buffer, sem, count):
         return pltpu.make_async_copy(
@@ -711,7 +715,7 @@
                 def _():
                     pltpu.make_async_remote_copy(
                         src_ref=own, dst_ref=upper.at[mine],
-                        send_sem=in_sem.at[len(SHARES) + 9], recv_sem=upper_recv,
+                        send_sem=in_sem.at[2 * len(RIMS)], recv_sem=upper_recv,
                         device_id={
                             "gx": me["gx"] - 1, "gy": turned["gy"][-target[0]],
                             "gz": turned["gz"][-target[1]],
@@ -916,7 +920,7 @@
 
     @pl.when(me["gx"] > 0)
     def _():
-        pltpu.make_async_copy(upper, upper, in_sem.at[len(SHARES) + 9]).wait()
+        pltpu.make_async_copy(upper, upper, in_sem.at[2 * len(RIMS)]).wait()
 
     for n, step in enumerate(RIMS):
         @pl.when(valid(step, -1))
@@ -1010,7 +1014,7 @@
         in_specs=jax.tree.map(lambda _: anywhere, operands),
         out_specs=in_vmem,
         scratch_shapes=[
-            like(right_side), like(iterate), like(coefficient), *[like(m) for m in matrices],
+            vmem(rhs, 2, nx, ny, nz), like(coefficient), *[like(m) for m in matrices],
             [like(m) for m in rows],
             pltpu.VMEM(mats[0].shape[1:], bf16), like(mats[1]),
             pltpu.VMEM(mats[2].shape[1:], bf16), like(mats[3]), like(mats[4]), like(mats[5]),
@@ -1051,7 +1055,7 @@
             [vmem(p, LANES) for p in gather_packs],
             vmem(PITCH, widths[1]),
             vmem(counts[0], PITCH, widths[1]),
-            dma(max(len(SHARES) + 10, 2 * rhs + len(operands) - 3)),
+            dma(max(len(SHARES) + 7, rhs + len(operands) - 3)),
             pltpu.SemaphoreType.REGULAR((2, max(peers["gx"] - 1, 1))),
             *[pltpu.SemaphoreType.DMA] * 2, dma(2), pltpu.SemaphoreType.DMA, dma(3), dma(1), dma(3), dma(2),
         ],

time: 27.8 us -> 27.8 us (level)
  no operation moved by 1% of the time
where the time goes in v6:
time: 27.8 us; the launch traced here: 27.7 us
  Pallas kernels  27.7 us (100%)
    pallas_call x1, Pallas kernels, per_device(): pl.pallas_call(functools.partial(kernel, sizes), out_shape=pltpu.VMEM(((s...  26.6 us
    pallas_call x1, Pallas kernels, per_device(): pl.pallas_call(spread_kernel, out_shape=jax.ShapeDtypeStruct(iterate.shap...  1.09 us

profile of v6, /device:TPU:0, one launch (start us, length us, event | category | flops | bytes accessed | tf_op | source)
XLA Modules:
  0.0 27.7 jit_solution(10225181287069712509)
XLA Ops:
  0.0 26.6 %shard_map.199.grown_ref = f32[168,96]{1,0:T(8,128)S(1)} custom-call(f32[4,24,24,24]{3,2,1,0:T(8,128)} %right_ref.1, f32[4,24,24,24]{3,2,1,0:T(8,128)} %u_ref.1, f32[24,24,24]{2,1,0:T(8,128)} %coef_ref.1, s32[1,216]{1,0:T(1,128)} %bitcast.29, f32[125,1,125]{2,1,0:T(1,128)} %bitcast.20, f32[50,1,125]{2,1,0:T(1,128)} %bitcast.24, f32[60,1,125]{2,1,0:T(1,128)} %bitcast.22, ...), custom_call_target="tpu_custom_call" | custom-call | tf_op jit(solution)/shard_map/pallas_call | solution.py:1011
  26.6 1.1 %shard_map.200 = f32[4,24,24,24]{3,2,1,0:T(8,128)} custom-call(f32[168,96]{1,0:T(8,128)S(1)} %shard_map.199.grown_ref), custom_call_target="tpu_custom_call" | custom-call | tf_op jit(solution)/shard_map/pallas_call | solution.py:1064
